TPU v7x, 32 devices: a whole 2x2x4 slice. The times are simulated.
32 devices in a mesh: dp: 4 (over x, y), ep: 8 (over z, core).
Axes of the slice: x: 2, y: 2, z: 4, core: 2. Of those that a mesh axis runs over, the one named last changes fastest.
Arguments:
- x: bfloat16 [4, 8, 256, 2048], P('dp', 'ep'), parts along dimension 0
- expert: int32 [4, 8, 256, 2], P('dp', 'ep'), parts along dimension 0
- slot: int32 [4, 8, 256, 2], P('dp', 'ep'), parts along dimension 0
- gate: float32 [4, 8, 256, 2], P('dp', 'ep'), parts along dimension 0
- w_gate: bfloat16 [8, 2048, 5632], P('ep')
- w_up: bfloat16 [8, 2048, 5632], P('ep')
- w_down: bfloat16 [8, 5632, 2048], P('ep')
Outputs:
- y: bfloat16 [4, 8, 256, 2048], P('dp', 'ep'), parts along dimension 0
There are 4 independent parts. A program takes and returns all parts, laid end to end along the dimension named above; an argument that names none is the same for every part.
All inputs are finite; a program needn't handle non-finite values.
Results may differ from a plain program's by a relative error of at most 0.009.
Values are sent between devices in bfloat16 or wider.
A program may use at most 2 GiB of HBM per device.

v0:
```python
import jax
import jax.numpy as jnp
from jax import lax
from jax.sharding import NamedSharding, PartitionSpec as P


def einsum(form, a, b):
    return jnp.einsum(form, a.astype(jnp.float32), b.astype(jnp.float32))


def solution(mesh):
    def placed(v, *spec):
        return lax.with_sharding_constraint(v, NamedSharding(mesh, P(*spec)))

    def step(x, expert, slot, gate, w_gate, w_up, w_down):
        experts, (tokens, top) = w_gate.shape[0], expert.shape[2:]
        slots = 5 * tokens * top // (4 * experts)
        to_expert = jax.nn.one_hot(expert, experts, dtype=jnp.bfloat16)
        to_slot = jax.nn.one_hot(slot, slots, dtype=jnp.bfloat16)
        weighted = to_expert * gate[..., None].astype(jnp.bfloat16)
        dispatch = einsum("abtke,abtkc->abtec", to_expert, to_slot).astype(jnp.bfloat16)
        combine = einsum("abtke,abtkc->abtec", weighted, to_slot).astype(jnp.bfloat16)
        z = einsum("abtec,abtd->aebcd", dispatch, x).astype(jnp.bfloat16)
        z = placed(z, "dp", None, "ep", None, None)
        z = placed(z, "dp", "ep", None, None, None)
        h = jax.nn.silu(einsum("aebcd,edf->aebcf", z, w_gate))
        h = (h * einsum("aebcd,edf->aebcf", z, w_up)).astype(jnp.bfloat16)
        out = einsum("aebcf,efd->aebcd", h, w_down).astype(jnp.bfloat16)
        out = placed(out, "dp", "ep", None, None, None)
        out = placed(out, "dp", None, "ep", None, None)
        y = einsum("abtec,aebcd->abtd", combine, out)
        return y.astype(jnp.bfloat16)

    return step
```

profile of v0, /device:TPU:1, one launch (start us, length us, event | category | flops | bytes accessed | tf_op | source)
XLA Modules:
  0.0 208.2 jit_solution(733514354059376726)
XLA Ops:
  0.0 0.0 copy-start
  0.0 0.9 copy.3
  0.9 0.8 copy.5
  1.7 1.8 fusion.39
  3.5 0.3 copy.9
  3.8 0.0 copy-done
  3.8 0.9 fusion.22
  4.7 65.4 %all-to-all.4 = bf16[1,8,1,1,80,2048]{5,4,3,2,0,1:T(8,128)(2,1)S(1)} all-to-all(bf16[1,8,1,1,80,2048]{5,4,3,2,0,1:T(8,128)(2,1)S(1)} %fusion.22), channel_id=1, replica_groups=mesh['dp'=4,'ep'=8] {'ep'}, dimensions={1} | all-to-all | bytes 5242880 | tf_op jit(solution)/sharding_constraint;jit(solution)/sharding_constraint | solution.py:13
  70.1 0.0 copy-start.2
  70.1 1.5 copy-done.2
  71.6 22.4 %fusion.4 = f32[8,80,5632]{2,1,0:T(8,128)} fusion(bf16[1,2048,5632]{2,1,0:T(8,128)(2,1)} %param.4, bf16[1,8,1,1,80,2048]{5,4,3,2,0,1:T(8,128)(2,1)S(1)} %all-to-all.4), kind=kOutput, calls=%fused_computation.4 | convolution fusion | flops 14763950080 | bytes 40108032 | tf_op jit(solution)/aebcd,edf->aebcf/dot_general | solution.py:8
  94.0 24.6 %fusion.12.clone.8 = bf16[8,80,5632]{2,1,0:T(8,128)(2,1)} fusion(bf16[1,2048,5632]{2,1,0:T(8,128)(2,1)} %param.5, f32[8,80,5632]{2,1,0:T(8,128)} %fusion.4, bf16[1,8,1,1,80,2048]{5,4,3,2,0,1:T(8,128)(2,1)} %copy-done.2), kind=kOutput, calls=%fused_computation.13.clone.clone.clone.clone.clone.clone.clone.1 | convolution fusion | flops 14785576960 | bytes 47316992 | tf_op jit(solution)/aebcd,edf->aebcf/dot_general | solution.py:8
  118.6 0.0 copy-start.3
  118.6 0.0 copy-start.1
  118.6 21.5 %fusion.23 = bf16[1,1,8,1,80,2048]{5,4,3,1,0,2:T(8,128)(2,1)} fusion(bf16[1,5632,2048]{2,1,0:T(8,128)(2,1)} %param.6, bf16[8,80,5632]{2,1,0:T(8,128)(2,1)} %fusion.12.clone.8), kind=kOutput, calls=%fused_computation.17 | convolution fusion | flops 14765260800 | bytes 32899072 | tf_op jit(solution)/aebcf,efd->aebcd/dot_general | solution.py:8
  140.1 5.4 %all-to-all-start.1 = ((bf16[1,1,8,1,80,2048]{5,4,3,1,0,2:T(8,128)(2,1)}), bf16[1,1,8,1,80,2048]{5,4,3,1,0,2:T(8,128)(2,1)}, u32[]{:S(2)}, u32[]{:S(2)}) async-start(bf16[1,1,8,1,80,2048]{5,4,3,1,0,2:T(8,128)(2,1)} %fusion.23), calls=%async_computation.1 | async-start | bytes 5242880 | tf_op jit(solution)/sharding_constraint;jit(solution)/sharding_constraint | solution.py:13
  145.5 0.0 copy-done.3
  145.5 0.1 copy.4
  145.6 2.2 %fusion.42 = bf16[256,8,80]{2,1,0:T(8,128)(2,1)S(1)} fusion(s32[256,2]{1,0:T(8,128)S(1)} %copy.5, s32[256,2]{1,0:T(8,128)S(1)} %copy.3, bf16[256,2]{1,0:T(8,128)(2,1)S(1)} %copy.4), kind=kOutput, calls=%fused_computation.28 | convolution fusion | flops 704512 | bytes 332800 | tf_op jit(solution)/abtke,abtkc->abtec/dot_general | solution.py:8
  147.8 0.3 copy.8
  148.2 56.3 %all-to-all-done.1 = bf16[1,1,8,1,80,2048]{5,4,3,1,0,2:T(8,128)(2,1)} async-done(((bf16[1,1,8,1,80,2048]{5,4,3,1,0,2:T(8,128)(2,1)}), bf16[1,1,8,1,80,2048]{5,4,3,1,0,2:T(8,128)(2,1)}, u32[]{:S(2)}, u32[]{:S(2)}) %all-to-all-start.1) | async-done | bytes 2621472 | tf_op jit(solution)/sharding_constraint;jit(solution)/sharding_constraint | solution.py:13
  204.5 3.7 %fusion.35 = bf16[1,1,256,2048]{3,2,1,0:T(8,128)(2,1)} fusion(bf16[1,1,8,1,80,2048]{5,4,3,1,0,2:T(8,128)(2,1)} %all-to-all-done.1, bf16[256,8,80]{0,2,1:T(8,128)(2,1)S(1)} %copy.8), kind=kOutput, calls=%fused_computation.23 | convolution fusion | flops 671612928 | bytes 3997696 | tf_op jit(solution)/abtec,aebcd->abtd/dot_general | solution.py:8
  208.2 0.0 copy-done.1
  (1 shorter events, 0.0 us)
Async XLA Ops:
  0.0 3.8 %copy-start = (bf16[1,1,256,2048]{3,2,1,0:T(8,128)(2,1)S(1)}, bf16[1,1,256,2048]{3,2,1,0:T(8,128)(2,1)}, u32[]{:S(2)}) copy-start(bf16[1,1,256,2048]{3,2,1,0:T(8,128)(2,1)} %param.3) | copy-start | bytes 3145732
  70.1 1.5 copy-start.2
  118.6 26.9 %copy-start.3 = (f32[1,1,256,2]{2,3,1,0:T(2,128)S(1)}, f32[1,1,256,2]{2,3,1,0:T(2,128)}, u32[]{:S(2)}) copy-start(f32[1,1,256,2]{2,3,1,0:T(2,128)} %param.1) | copy-start | bytes 6148
  118.6 89.7 %copy-start.1 = (bf16[1,1,256,2048]{3,2,1,0:T(8,128)(2,1)S(1)}, bf16[1,1,256,2048]{3,2,1,0:T(8,128)(2,1)}, u32[]{:S(2)}) copy-start(bf16[1,1,256,2048]{3,2,1,0:T(8,128)(2,1)} %param.3) | copy-start | bytes 3145732
  140.1 64.4 %all-to-all-start.1 = ((bf16[1,1,8,1,80,2048]{5,4,3,1,0,2:T(8,128)(2,1)}), bf16[1,1,8,1,80,2048]{5,4,3,1,0,2:T(8,128)(2,1)}, u32[]{:S(2)}, u32[]{:S(2)}) async-start(bf16[1,1,8,1,80,2048]{5,4,3,1,0,2:T(8,128)(2,1)} %fusion.23), calls=%async_computation.1 | async-start | bytes 5242880 | tf_op jit(solution)/sharding_constraint;jit(solution)/sharding_constraint | solution.py:13
where the time goes:
time: 210 us; the launch traced here: 208 us
  matrix products  77 us (37%)
  blocking collectives  65.4 us (31%)
  waiting for transfers between devices  56.3 us (27%)
  starting transfers between devices  5.41 us (3%)
  local copies, waits for them, and re-layouts  4.05 us (2%)
    dot_general x7, matrix products, einsum(): return jnp.einsum(form, a.astype(jnp.float32), b.astype(jnp.float32))  77 us
    another operation x1, blocking collectives, placed(): return lax.with_sharding_constraint(v, NamedSharding(mesh, P(*spec)))  65.4 us
    another operation x1, waiting for transfers between devices, placed(): return lax.with_sharding_constraint(v, NamedSharding(mesh, P(*spec)))  56.3 us
    another operation x1, starting transfers between devices, placed(): return lax.with_sharding_constraint(v, NamedSharding(mesh, P(*spec)))  5.41 us
  transfers between devices with their start and end apart: 1, of which 1 were waited for; matrix products, arithmetic and copies ran while one was open for 1% of the time, Pallas kernels for 0%

commit v1 on v0

v1 whole, which is shorter than its diff:
```python
import functools

import jax
import jax.numpy as jnp
from jax import lax
from jax.experimental import pallas as pl
from jax.experimental.pallas import tpu as pltpu
from jax.sharding import PartitionSpec as P

MESH = pl.DeviceIdType.MESH
F32, BF16 = jnp.float32, jnp.bfloat16
PIECES = 4
GU_TILES = 11
DN_TILES = 8
NBUF = 4


def kernel(slots, meta, x_hbm, wg, wu, wd, y_hbm,
           xv, xf, mf, oh, za, zb, stage, stagef, hbuf, oa, ob_, ro, rof,
           part, prt, yv, gbuf, ubuf, dbuf,
           xsem, gsem, usem, dsem, ysem, go,
           s_meta, s_x, s_own, s_rel, s_outa, s_outb, s_part,
           r_meta, r_x, r_za, r_zp, r_zb, r_zn, r_rof, r_ro, r_part):
    S = slots
    T, D = xv.shape
    FT = gbuf.shape[-1]
    NT = dbuf.shape[-1]
    C = D // PIECES
    HALF = 4 * S

    dp = lax.axis_index("dp")
    me = lax.axis_index("ep")
    z = lax.div(me, 2)
    k = lax.rem(me, 2)
    h = lax.div(me, 4)
    q = lax.rem(me, 4)
    mid = lax.rem(z + h, 2) == 1
    end = lax.rem(z + h, 2) == 0
    partner = 2 * z + 1 - k
    qp = partner - 4 * h
    other = 2 + 8 * h - 2 * z
    qo = other - 4 * h
    relay = 4 - 2 * h + k
    far_end = 6 - 6 * h + k
    base = h * HALF

    def rows(i):
        return pl.ds(pl.multiple_of(i * S, 16), S)

    def cols(p):
        return pl.ds(pl.multiple_of(p * C, 128), C)

    def send(src, dst, ssem, rsem, dev):
        return pltpu.make_async_remote_copy(
            src_ref=src, dst_ref=dst, send_sem=ssem, recv_sem=rsem,
            device_id=(dp, dev), device_id_type=MESH)

    def recv(dst, rsem):
        pltpu.make_async_remote_copy(
            src_ref=dst, dst_ref=dst, send_sem=rsem, recv_sem=rsem,
            device_id=(dp, partner), device_id_type=MESH).wait_recv()

    def gu_copies(t):
        slot = lax.rem(t, NBUF)
        tile = pl.ds(pl.multiple_of(lax.rem(t, GU_TILES) * FT, 128), FT)
        return (pltpu.make_async_copy(wg.at[:, tile], gbuf.at[slot], gsem.at[slot]),
                pltpu.make_async_copy(wu.at[:, tile], ubuf.at[slot], usem.at[slot]))

    def dn_copy(t):
        slot = lax.rem(t, NBUF)
        tile = pl.ds(pl.multiple_of(lax.rem(t, DN_TILES) * NT, 128), NT)
        return pltpu.make_async_copy(wd.at[:, tile], dbuf.at[slot], dsem.at[slot])

    xload = [pltpu.make_async_copy(x_hbm.at[:, cols(p)], xv.at[:, cols(p)], xsem.at[p])
             for p in range(PIECES)]
    for c in xload:
        c.start()
    for t in range(NBUF):
        for c in gu_copies(jnp.int32(t)):
            c.start()
    for t in range(NBUF):
        dn_copy(jnp.int32(t)).start()

    barrier = pltpu.get_barrier_semaphore()
    for d in range(1, 8):
        pl.semaphore_signal(barrier, inc=1, device_id=(dp, lax.rem(me + d, 8)), device_id_type=MESH)

    def onehot(m):
        idx = m[...].astype(jnp.int32) - base
        r = lax.broadcasted_iota(jnp.int32, (HALF, T), 0)
        hit = (r == idx[0:1, :]) | (r == idx[1:2, :])
        return jnp.where(hit, 1.0, 0.0).astype(BF16)

    def weights_of(m):
        mt = jnp.transpose(jnp.concatenate([m[...], jnp.zeros((120, T), F32)], axis=0))
        idx = mt.astype(jnp.int32) - base
        r = lax.broadcasted_iota(jnp.int32, (T, HALF), 1)
        w = jnp.where(r == idx[:, 0:1], mt[:, 2:3], 0.0)
        w = jnp.where(r == idx[:, 1:2], mt[:, 3:4], w)
        return w.astype(BF16)

    def dot(a, b):
        return jnp.dot(a, b, preferred_element_type=F32)

    oh[0] = onehot(meta)
    pl.semaphore_wait(barrier, 7)

    side = lax.rem(z + h + 1, 2)

    def send_x(p):
        return send(xv.at[:, cols(p)], xf.at[side, :, cols(p)], s_x.at[p], r_x.at[side, p], relay)

    def own_copies(p):
        a = send(stage.at[rows(qp), cols(p)], za.at[rows(2 + k), cols(p)], s_own.at[0, p], r_zp.at[p], partner)
        b = [send(stage.at[rows(qo + j), cols(p)], zb.at[rows(2 + k), cols(p)], s_own.at[1 + j, p],
                  r_zn.at[k, p], other + j) for j in range(2)]
        return a, b

    send_meta = send(meta, mf.at[side], s_meta, r_meta.at[side], relay)
    send_meta.start()
    for p in range(PIECES):
        xload[p].wait()

        @pl.when(mid)
        def _(p=p):
            send_x(p).start()

    for p in range(PIECES):
        stage[:, cols(p)] = dot(oh[0], xv[:, cols(p)]).astype(BF16)
        za[rows(2 + k), cols(p)] = stage[rows(q), cols(p)]
        a, b = own_copies(p)
        a.start()
        if p < 2:
            for c in b:
                c.start()
        else:
            @pl.when(end)
            def _(b=b):
                for c in b:
                    c.start()

    def relay_copies(f, p):
        zx = za if f == 0 else zb
        rz = r_za if f == 0 else r_zb
        return [send(stagef.at[f, rows(qd), cols(p)], zx.at[rows(k), cols(p)], s_rel.at[f, j, p],
                     rz.at[k, p], dev)
                for j, (qd, dev) in enumerate(((qo, other), (qo + 1, other + 1), (qp, partner)))]

    def relay_piece(f, p):
        zx = za if f == 0 else zb
        recv(xf.at[f, :, cols(p)], r_x.at[f, p])
        stagef[f, :, cols(p)] = dot(oh[1 + f], xf[f, :, cols(p)]).astype(BF16)
        for c in relay_copies(f, p):
            c.start()
        zx[rows(k), cols(p)] = stagef[f, rows(q), cols(p)]

    def relay_head(f):
        recv(mf.at[f], r_meta.at[f])
        oh[1 + f] = onehot(mf.at[f])

    @pl.when(mid)
    def _():
        relay_head(0)
        for p in range(PIECES):
            relay_piece(0, p)
            if p == PIECES - 2:
                pl.semaphore_signal(go, inc=1, device_id=(dp, far_end), device_id_type=MESH)
        for p in range(2, PIECES):
            for c in own_copies(p)[1]:
                c.start()

    @pl.when(end)
    def _():
        pl.semaphore_wait(go, 1)
        for p in range(PIECES):
            send_x(p).start()
        for p in range(PIECES):
            recv(za.at[rows(k), cols(p)], r_za.at[k, p])

    for p in range(PIECES):
        recv(za.at[rows(1 - k), cols(p)], r_za.at[1 - k, p])
        recv(za.at[rows(3 - k), cols(p)], r_zp.at[p])

    def gu_tile(zx, t, i):
        for c in gu_copies(t):
            c.wait()
        slot = lax.rem(t, NBUF)

        @pl.when((t >= 1) & (t + NBUF - 1 < 2 * GU_TILES))
        def _():
            for c in gu_copies(t + NBUF - 1):
                c.start()

        g = dot(zx[...], gbuf[slot])
        u = dot(zx[...], ubuf[slot])
        hbuf[:, pl.ds(pl.multiple_of(i * FT, 128), FT)] = (g * jax.nn.sigmoid(g) * u).astype(BF16)

    def dn_tile(ox, t, n):
        dn_copy(t).wait()
        slot = lax.rem(t, NBUF)

        @pl.when((t >= 1) & (t + NBUF - 1 < 2 * DN_TILES))
        def _():
            dn_copy(t + NBUF - 1).start()

        ox[:, pl.ds(pl.multiple_of(n * NT, 128), NT)] = dot(hbuf[...], dbuf[slot]).astype(BF16)

    def out_far(f, p, start):
        ox = oa if f == 0 else ob_
        ss = s_outa if f == 0 else s_outb

        def to(kk, dev):
            return send(ox.at[rows(kk), cols(p)], rof.at[f, rows(q), cols(p)], ss.at[kk, p],
                        r_rof.at[f, q, p], dev)

        @pl.when(mid)
        def _():
            c = to(1 - k, partner)
            if start:
                c.start()
                rof[f, rows(q), cols(p)] = ox[rows(k), cols(p)]
            else:
                c.wait_send()

        @pl.when(end)
        def _():
            for kk in range(2):
                c = to(kk, other + kk)
                c.start() if start else c.wait_send()

    def out_near_a(p):
        return send(oa.at[rows(3 - k), cols(p)], ro.at[rows(q), cols(p)], s_outa.at[2, p], r_ro.at[q, p], partner)

    def out_near_b(p):
        return [send(ob_.at[rows(2 + j), cols(p)], ro.at[rows(q), cols(p)], s_outb.at[2 + j, p],
                     r_ro.at[q, p], other + j) for j in range(2)]

    def send_part(f, p):
        dev = relay if f == 0 else far_end
        return send(prt.at[f, :, cols(p)], part.at[:, cols(p)], s_part.at[f, p], r_part.at[p], dev)

    def combine_piece(f, p):
        for qq in (qp, qo, qo + 1):
            recv(rof.at[f, rows(qq), cols(p)], r_rof.at[f, qq, p])
        prt[f, :, cols(p)] = dot(weights_of(mf.at[f]), rof[f, :, cols(p)]).astype(BF16)
        send_part(f, p).start()

    @pl.loop(0, GU_TILES)
    def _(i):
        gu_tile(za, i, i)

        @pl.when(mid & (i == 2))
        def _():
            relay_head(1)

        @pl.when(mid & (lax.rem(i, 4) == 3))
        def _():
            relay_piece(1, lax.div(i, 4))

    @pl.loop(0, DN_TILES)
    def _(n):
        @pl.when(mid & (lax.rem(n, 5) == 0))
        def _():
            relay_piece(1, 2 + lax.div(n, 5))

        dn_tile(oa, n, n)

        @pl.when(lax.rem(n, 2) == 1)
        def _():
            p = lax.div(n, 2)
            out_far(0, p, True)
            out_near_a(p).start()
            ro[rows(q), cols(p)] = oa[rows(2 + k), cols(p)]

    @pl.when(end)
    def _():
        for p in range(PIECES):
            recv(zb.at[rows(k), cols(p)], r_zb.at[k, p])

    for p in range(PIECES):
        recv(zb.at[rows(1 - k), cols(p)], r_zb.at[1 - k, p])
        for j in range(2):
            recv(zb.at[rows(2 + j), cols(p)], r_zn.at[j, p])

    @pl.loop(0, GU_TILES)
    def _(i):
        @pl.when(mid & (lax.rem(i, 3) == 0))
        def _():
            combine_piece(0, lax.div(i, 3))

        gu_tile(zb, GU_TILES + i, i)

    @pl.loop(0, DN_TILES)
    def _(n):
        dn_tile(ob_, DN_TILES + n, n)

        @pl.when(lax.rem(n, 2) == 1)
        def _():
            out_far(1, lax.div(n, 2), True)

    for p in range(PIECES):
        for c in out_near_b(p):
            c.start()

    @pl.when(mid)
    def _():
        for p in range(PIECES):
            combine_piece(1, p)

    ycopy = [pltpu.make_async_copy(yv.at[:, cols(p)], y_hbm.at[:, cols(p)], ysem.at[p]) for p in range(PIECES)]
    w_own = weights_of(meta)
    for p in range(PIECES):
        recv(ro.at[rows(qp), cols(p)], r_ro.at[qp, p])
        for j in range(2):
            recv(ro.at[rows(qo + j), cols(p)], r_ro.at[qo + j, p])
        recv(part.at[:, cols(p)], r_part.at[p])
        yv[:, cols(p)] = (dot(w_own, ro[:, cols(p)]) + part[:, cols(p)].astype(F32)).astype(BF16)
        ycopy[p].start()

    send_meta.wait_send()
    for p in range(PIECES):
        send_x(p).wait_send()
        a, b = own_copies(p)
        for c in (a, *b, out_near_a(p), *out_near_b(p)):
            c.wait_send()
        for f in range(2):
            out_far(f, p, False)

    @pl.when(mid)
    def _():
        for p in range(PIECES):
            for f in range(2):
                for c in relay_copies(f, p):
                    c.wait_send()
                send_part(f, p).wait_send()

    for c in ycopy:
        c.wait()


def solution(mesh):
    def step(x, expert, slot, gate, w_gate, w_up, w_down):
        tokens, depth = x.shape[2:]
        ff = w_gate.shape[2]
        top = expert.shape[3]
        slots = 5 * tokens * top // (4 * 8)
        place = jnp.where(slot < slots, expert * slots + slot, -100000).astype(F32)
        meta = jnp.concatenate([place.reshape(tokens, top), gate.reshape(tokens, top),
                                jnp.zeros((tokens, 8 - 2 * top), F32)], axis=1).T
        half = 4 * slots
        dma = pltpu.SemaphoreType.DMA
        vmem = pltpu.VMEM
        hbm = pl.BlockSpec(memory_space=pl.ANY)
        y = pl.pallas_call(
            functools.partial(kernel, slots),
            out_shape=jax.ShapeDtypeStruct((tokens, depth), BF16),
            in_specs=[pl.BlockSpec(memory_space=pltpu.VMEM)] + [hbm] * 4,
            out_specs=hbm,
            scratch_shapes=[
                vmem((tokens, depth), BF16),
                vmem((2, tokens, depth), BF16),
                vmem((2, 8, tokens), F32),
                vmem((3, half, tokens), BF16),
                vmem((half, depth), BF16),
                vmem((half, depth), BF16),
                vmem((half, depth), BF16),
                vmem((2, half, depth), BF16),
                vmem((half, ff), BF16),
                vmem((half, depth), BF16),
                vmem((half, depth), BF16),
                vmem((half, depth), BF16),
                vmem((2, half, depth), BF16),
                vmem((tokens, depth), BF16),
                vmem((2, tokens, depth), BF16),
                vmem((tokens, depth), BF16),
                vmem((NBUF, depth, ff // GU_TILES), BF16),
                vmem((NBUF, depth, ff // GU_TILES), BF16),
                vmem((NBUF, ff, depth // DN_TILES), BF16),
                dma((PIECES,)), dma((NBUF,)), dma((NBUF,)), dma((NBUF,)), dma((PIECES,)),
                pltpu.SemaphoreType.REGULAR,
                dma, dma((PIECES,)), dma((3, PIECES)), dma((2, 3, PIECES)),
                dma((3, PIECES)), dma((4, PIECES)), dma((2, PIECES)),
                dma((2,)), dma((2, PIECES)), dma((2, PIECES)), dma((PIECES,)),
                dma((2, PIECES)), dma((2, PIECES)), dma((2, 4, PIECES)), dma((4, PIECES)), dma((PIECES,)),
            ],
            compiler_params=pltpu.CompilerParams(
                collective_id=0, has_side_effects=True, vmem_limit_bytes=67043328),
        )(meta, x.reshape(tokens, depth), w_gate[0], w_up[0], w_down[0])
        return y.reshape(x.shape)

    tok = P("dp", "ep")
    return jax.shard_map(step, mesh=mesh, in_specs=(tok,) * 4 + (P("ep"),) * 3, out_specs=tok, check_vma=False)
```

time: 210 us -> 155 us (0.74)
  Pallas kernels: 0 us -> 150 us
  matrix products: 77 us -> 0 us
  blocking collectives: 65.4 us -> 0 us
  waiting for transfers between devices: 56.3 us -> 0 us
  starting transfers between devices: 5.41 us -> 0 us
    pallas_call x0 -> x1, Pallas kernels: none -> 150 us  [step(): pl.pallas_call(functools.partial(kernel, slots), out_shape=jax.ShapeDtype...]
    dot_general x7 -> x0, matrix products: 77 us -> none  [einsum(): return jnp.einsum(form, a.astype(jnp.float32), b.astype(jnp.float32))]
    another operation x1 -> x0, blocking collectives: 65.4 us -> none  [placed(): return lax.with_sharding_constraint(v, NamedSharding(mesh, P(*spec)))]
    another operation x1 -> x0, waiting for transfers between devices: 56.3 us -> none  [placed(): return lax.with_sharding_constraint(v, NamedSharding(mesh, P(*spec)))]
    another operation x1 -> x0, starting transfers between devices: 5.41 us -> none  [placed(): return lax.with_sharding_constraint(v, NamedSharding(mesh, P(*spec)))]
  transfers between devices with their start and end apart: 1 -> 0, of which waited for: 1 -> 0; matrix products, arithmetic and copies ran while one was open for 1% -> 0% of each run, Pallas kernels for 0% -> 0%
where the time goes in v1:
time: 155 us
  Pallas kernels  150 us (97%)
  local copies, waits for them, and re-layouts  2.38 us (2%)
  other arithmetic  2.05 us (1%)
    pallas_call x1, Pallas kernels, step(): pl.pallas_call(functools.partial(kernel, slots), out_shape=jax.ShapeDtype...  150 us

profile of v1, /device:TPU:1, one launch (start us, length us, event | category | flops | bytes accessed | tf_op | source)
XLA Modules:
  0.0 154.7 jit_solution(10837960111591493399)
XLA Ops:
  0.0 0.1 pad.2.clone
  0.1 0.7 fusion.1
  0.8 1.3 maximum_bitcast_fusion.meta
  2.1 150.2 %shard_map.73 = bf16[256,2048]{1,0:T(8,128)(2,1)} custom-call(f32[8,256]{1,0:T(8,128)} %maximum_bitcast_fusion.meta, bf16[256,2048]{1,0:T(8,128)(2,1)} %bitcast.14, bf16[2048,5632]{1,0:T(8,128)(2,1)} %bitcast.10, bf16[2048,5632]{1,0:T(8,128)(2,1)} %bitcast.11, bf16[5632,2048]{1,0:T(8,128)(2,1)} %bitcast.12), custom_call_target="tpu_custom_call" | custom-call | tf_op jit(solution)/shard_map/pallas_call | solution.py:354
  152.4 2.3 %copy.9 = bf16[1,1,256,2048]{3,2,1,0:T(8,128)(2,1)} copy(bf16[1,1,256,2048]{3,2,1,0:T(8,128)(2,1)} %bitcast.13) | data formatting | bytes 2097152
  (1 shorter events, 0.0 us)

commit v2 on v1

v2 whole, which is shorter than its diff:
```python
import functools

import jax
import jax.numpy as jnp
from jax import lax
from jax.experimental import pallas as pl
from jax.experimental.pallas import tpu as pltpu
from jax.sharding import PartitionSpec as P

MESH = pl.DeviceIdType.MESH
F32, BF16 = jnp.float32, jnp.bfloat16
PIECES = 4
NBUF = 4
DBUF = 2


def kernel(slots, expert, slot, gate, x_hbm, wg, wu, wd, y_hbm,
           meta, xv, xf, mf, oh, wt, za, zb, stage, stagef, acc, hbuf, ro, rof,
           part, kbuf, dbuf,
           xsem, ksem, dsem, ysem, go,
           s_meta, s_x, s_own, s_rel, s_outa, s_outb, s_part,
           r_meta, r_x, r_za, r_zp, r_zn, r_zb, r_rof, r_ro, r_part):
    S = slots
    T, D = xv.shape
    FF = hbuf.shape[1]
    KT, FT = kbuf.shape[1:]
    NT = dbuf.shape[2]
    C = D // PIECES
    HALF = 4 * S
    NF = FF // FT
    GU = 2 * NF * PIECES

    dp = lax.axis_index("dp")
    me = lax.axis_index("ep")
    z = lax.div(me, 2)
    k = lax.rem(me, 2)
    h = lax.div(me, 4)
    q = lax.rem(me, 4)
    side = lax.rem(z + h + 1, 2)
    mid = side == 0
    end = side == 1
    partner = 2 * z + 1 - k
    qp = partner - 4 * h
    other = 2 + 8 * h - 2 * z
    qo = other - 4 * h
    relay = 4 - 2 * h + k
    far_end = 6 - 6 * h + k
    base = h * HALF

    def rows(i):
        return pl.ds(pl.multiple_of(i * S, 16), S)

    def cols(p):
        return pl.ds(pl.multiple_of(p * C, 128), C)

    def send(src, dst, ssem, rsem, dev):
        return pltpu.make_async_remote_copy(
            src_ref=src, dst_ref=dst, send_sem=ssem, recv_sem=rsem,
            device_id=(dp, dev), device_id_type=MESH)

    def recv(dst, rsem):
        pltpu.make_async_remote_copy(
            src_ref=dst, dst_ref=dst, send_sem=rsem, recv_sem=rsem,
            device_id=(dp, partner), device_id_type=MESH).wait_recv()

    def gu_copy(t, w, m):
        t = lax.rem(t, GU)
        r = pl.ds(pl.multiple_of(lax.div(t, 2 * NF) * KT, 128), KT)
        c = pl.ds(pl.multiple_of(lax.div(lax.rem(t, 2 * NF), 2) * FT, 128), FT)
        return w.at[r, c]

    def gu_start(t):
        s = lax.rem(t, NBUF)

        @pl.when(lax.rem(t, 2) == 0)
        def _():
            pltpu.make_async_copy(gu_copy(t, wg, 0), kbuf.at[s], ksem.at[s]).start()

        @pl.when(lax.rem(t, 2) == 1)
        def _():
            pltpu.make_async_copy(gu_copy(t, wu, 1), kbuf.at[s], ksem.at[s]).start()

    def gu_wait(t):
        s = lax.rem(t, NBUF)
        pltpu.make_async_copy(gu_copy(t, wg, 0), kbuf.at[s], ksem.at[s]).wait()
        return s

    def dn_copy(t):
        s = lax.rem(t, DBUF)
        tile = pl.ds(pl.multiple_of(lax.rem(t, PIECES) * NT, 128), NT)
        return pltpu.make_async_copy(wd.at[:, tile], dbuf.at[s], dsem.at[s])

    xload = [pltpu.make_async_copy(x_hbm.at[:, cols(p)], xv.at[:, cols(p)], xsem.at[p])
             for p in range(PIECES)]
    for c in xload:
        c.start()
    for t in range(NBUF):
        gu_start(jnp.int32(t))
    for t in range(DBUF):
        dn_copy(jnp.int32(t)).start()

    barrier = pltpu.get_barrier_semaphore()
    for d in range(1, 8):
        pl.semaphore_signal(barrier, inc=1, device_id=(dp, lax.rem(me + d, 8)), device_id_type=MESH)

    def onehot(m):
        idx = m[...].astype(jnp.int32) - base
        r = lax.broadcasted_iota(jnp.int32, (HALF, T), 0)
        hit = (r == idx[0:1, :]) | (r == idx[1:2, :])
        return jnp.where(hit, 1.0, 0.0).astype(BF16)

    def weights_of(m):
        mt = jnp.transpose(jnp.concatenate([m[...], jnp.zeros((120, T), F32)], axis=0))
        idx = mt.astype(jnp.int32) - base
        r = lax.broadcasted_iota(jnp.int32, (T, HALF), 1)
        w = jnp.where(r == idx[:, 0:1], mt[:, 2:3], 0.0)
        w = jnp.where(r == idx[:, 1:2], mt[:, 3:4], w)
        return w.astype(BF16)

    def dot(a, b):
        return jnp.dot(a, b, preferred_element_type=F32)

    meta[...] = jnp.zeros_like(meta)
    meta[0:2, :] = jnp.where(slot[...] < S, expert[...] * S + slot[...], -100000).astype(F32)
    meta[2:4, :] = gate[...]
    oh[0] = onehot(meta)
    wt[0] = weights_of(meta)
    pl.semaphore_wait(barrier, 7)

    send_meta = send(meta, mf.at[side], s_meta, r_meta.at[side], relay)

    def send_x(p):
        return send(xv.at[:, cols(p)], xf.at[side, :, cols(p)], s_x.at[p], r_x.at[side, p], relay)

    def own_copies(p):
        a = send(stage.at[rows(qp), cols(p)], zb.at[rows(2 + k), cols(p)], s_own.at[0, p], r_zp.at[p], partner)
        b = [send(stage.at[rows(qo + j), cols(p)], za.at[rows(2 + k), cols(p)], s_own.at[1 + j, p],
                  r_zn.at[k, p], other + j) for j in range(2)]
        return a, b

    send_meta.start()
    for p in range(PIECES):
        xload[p].wait()

        @pl.when(mid)
        def _(p=p):
            send_x(p).start()

    for p in range(PIECES):
        stage[:, cols(p)] = dot(oh[0], xv[:, cols(p)]).astype(BF16)
        a, b = own_copies(p)
        if p < 2:
            for c in b:
                c.start()
        else:
            @pl.when(end)
            def _(b=b):
                for c in b:
                    c.start()
        a.start()
        zb[rows(2 + k), cols(p)] = stage[rows(q), cols(p)]

    def relay_copies(f, p):
        zx, rz = (za, r_za) if f == 0 else (zb, r_zb)
        return [send(stagef.at[f, rows(qd), cols(p)], zx.at[rows(k), cols(p)], s_rel.at[f, j, p],
                     rz.at[k, p], dev)
                for j, (qd, dev) in enumerate(((qo, other), (qo + 1, other + 1), (qp, partner)))]

    def relay_piece(f, p):
        zx = za if f == 0 else zb
        if p == 0:
            recv(mf.at[f], r_meta.at[f])
            oh[1 + f] = onehot(mf.at[f])
        recv(xf.at[f, :, cols(p)], r_x.at[f, p])
        stagef[f, :, cols(p)] = dot(oh[1 + f], xf[f, :, cols(p)]).astype(BF16)
        for c in relay_copies(f, p):
            c.start()
        zx[rows(k), cols(p)] = stagef[f, rows(q), cols(p)]
        if p == PIECES - 1:
            wt[1 + f] = weights_of(mf.at[f])

    def await_z(f, p):
        zx, rz = (za, r_za) if f == 0 else (zb, r_zb)

        @pl.when(end)
        def _():
            recv(zx.at[rows(k), cols(p)], rz.at[k, p])

        recv(zx.at[rows(1 - k), cols(p)], rz.at[1 - k, p])
        if f == 0:
            for j in range(2):
                recv(za.at[rows(2 + j), cols(p)], r_zn.at[j, p])
        else:
            recv(zb.at[rows(3 - k), cols(p)], r_zp.at[p])

    def ft(c):
        return pl.ds(pl.multiple_of(c * FT, 128), FT)

    def gu_next(t):
        @pl.when(t + NBUF < 2 * GU)
        def _():
            gu_start(t + NBUF)

    def gu_piece(f, p, hooks=()):
        zx = za if f == 0 else zb
        t0 = f * GU + p * 2 * NF
        zp = zx.at[:, cols(p)]
        if p < PIECES - 1:
            @pl.loop(0, 2 * NF)
            def _(i):
                for at, fn in hooks:
                    pl.when(mid & (i == at))(fn)
                s = gu_wait(t0 + i)
                m, c = lax.rem(i, 2), ft(lax.div(i, 2))
                if p == 0:
                    acc[m, :, c] = dot(zp[...], kbuf[s])
                else:
                    acc[m, :, c] += dot(zp[...], kbuf[s])
                gu_next(t0 + i)
        else:
            @pl.loop(0, NF)
            def _(i):
                for at, fn in hooks:
                    pl.when(mid & (i == at))(fn)
                c = ft(i)
                s = gu_wait(t0 + 2 * i)
                g = acc[0, :, c] + dot(zp[...], kbuf[s])
                acc[0, :, c] = g * jax.nn.sigmoid(g)
                gu_next(t0 + 2 * i)
                s = gu_wait(t0 + 2 * i + 1)
                hbuf[:, c] = (acc[0, :, c] * (acc[1, :, c] + dot(zp[...], kbuf[s]))).astype(BF16)
                gu_next(t0 + 2 * i + 1)

    def dn_piece(f, p):
        ox = za if f == 0 else zb
        t = f * PIECES + p
        dn_copy(t).wait()
        ox[:, cols(p)] = dot(hbuf[...], dbuf[lax.rem(t, DBUF)]).astype(BF16)

        @pl.when(t + DBUF < 2 * PIECES)
        def _():
            dn_copy(t + DBUF).start()

    def out_far(f, p, start):
        ox = za if f == 0 else zb
        ss = s_outa if f == 0 else s_outb

        def to(kk, dev):
            return send(ox.at[rows(kk), cols(p)], rof.at[f, rows(q), cols(p)], ss.at[kk, p],
                        r_rof.at[f, q, p], dev)

        @pl.when(mid)
        def _():
            c = to(1 - k, partner)
            if start:
                c.start()
                rof[f, rows(q), cols(p)] = ox[rows(k), cols(p)]
            else:
                c.wait_send()

        @pl.when(end)
        def _():
            for kk in range(2):
                c = to(kk, other + kk)
                c.start() if start else c.wait_send()

    def out_near_a(p):
        return [send(za.at[rows(2 + j), cols(p)], ro.at[rows(q), cols(p)], s_outa.at[2 + j, p],
                     r_ro.at[q, p], other + j) for j in range(2)]

    def out_near_b(p):
        return send(zb.at[rows(3 - k), cols(p)], ro.at[rows(q), cols(p)], s_outb.at[2, p], r_ro.at[q, p], partner)

    def send_part(f, p):
        dev = relay if f == 0 else far_end
        return send(xf.at[f, :, cols(p)], part.at[:, cols(p)], s_part.at[f, p], r_part.at[p], dev)

    def combine_piece(f, p):
        for qq in (qp, qo, qo + 1):
            recv(rof.at[f, rows(qq), cols(p)], r_rof.at[f, qq, p])
        xf[f, :, cols(p)] = dot(wt[1 + f], rof[f, :, cols(p)]).astype(BF16)
        send_part(f, p).start()

    for p in range(PIECES):
        @pl.when(mid)
        def _(p=p):
            relay_piece(0, p)
            if p + 2 < PIECES:
                for c in own_copies(p + 2)[1]:
                    c.start()
            if p == 1:
                pl.semaphore_signal(go, inc=1, device_id=(dp, far_end), device_id_type=MESH)

        if p == 2:
            @pl.when(end)
            def _():
                pl.semaphore_wait(go, 1)
                for pp in range(PIECES):
                    send_x(pp).start()

        await_z(0, p)
        gu_piece(0, p)

    @pl.loop(0, PIECES)
    def _(p):
        @pl.when(mid & (p == 0))
        def _():
            relay_piece(1, 0)

        @pl.when(mid & (p == 3))
        def _():
            relay_piece(1, 1)

        dn_piece(0, p)
        out_far(0, p, True)

    for p in range(PIECES):
        for c in out_near_a(p):
            c.start()

    hooks = {1: ((3, 0),), 2: ((2, 1),), 3: ((0, 2), (1, 3))}
    for p in range(PIECES):
        @pl.when(mid)
        def _(p=p):
            if p + 1 >= 2 and p + 1 < PIECES:
                relay_piece(1, p + 1)

        await_z(1, p)
        gu_piece(1, p, [(at, functools.partial(combine_piece, 0, pp)) for at, pp in hooks.get(p, ())])

    @pl.loop(0, PIECES)
    def _(p):
        dn_piece(1, p)
        out_far(1, p, True)
        out_near_b(p).start()
        ro[rows(q), cols(p)] = zb[rows(2 + k), cols(p)]

    @pl.when(mid)
    def _():
        for p in range(PIECES):
            combine_piece(1, p)

    send_meta.wait_send()
    for p in range(PIECES):
        send_x(p).wait_send()
    ycopy = [pltpu.make_async_copy(xv.at[:, cols(p)], y_hbm.at[:, cols(p)], ysem.at[p]) for p in range(PIECES)]
    for p in range(PIECES):
        recv(ro.at[rows(qp), cols(p)], r_ro.at[qp, p])
        for j in range(2):
            recv(ro.at[rows(qo + j), cols(p)], r_ro.at[qo + j, p])
        recv(part.at[:, cols(p)], r_part.at[p])
        xv[:, cols(p)] = (dot(wt[0], ro[:, cols(p)]) + part[:, cols(p)].astype(F32)).astype(BF16)
        ycopy[p].start()

    for p in range(PIECES):
        a, b = own_copies(p)
        for c in (a, *b, *out_near_a(p), out_near_b(p)):
            c.wait_send()
        for f in range(2):
            out_far(f, p, False)

    @pl.when(mid)
    def _():
        for p in range(PIECES):
            for f in range(2):
                for c in relay_copies(f, p):
                    c.wait_send()
                send_part(f, p).wait_send()

    for c in ycopy:
        c.wait()


def solution(mesh):
    def step(x, expert, slot, gate, w_gate, w_up, w_down):
        tokens, depth = x.shape[2:]
        ff = w_gate.shape[2]
        top = expert.shape[3]
        slots = 5 * tokens * top // (4 * 8)
        half = 4 * slots
        dma = pltpu.SemaphoreType.DMA
        vmem = pltpu.VMEM
        hbm = pl.BlockSpec(memory_space=pl.ANY)
        y = pl.pallas_call(
            functools.partial(kernel, slots),
            out_shape=jax.ShapeDtypeStruct((tokens, depth), BF16),
            in_specs=[pl.BlockSpec(memory_space=pltpu.VMEM)] * 3 + [hbm] * 4,
            out_specs=hbm,
            scratch_shapes=[
                vmem((8, tokens), F32),
                vmem((tokens, depth), BF16),
                vmem((2, tokens, depth), BF16),
                vmem((2, 8, tokens), F32),
                vmem((3, half, tokens), BF16),
                vmem((3, tokens, half), BF16),
                vmem((half, depth), BF16),
                vmem((half, depth), BF16),
                vmem((half, depth), BF16),
                vmem((2, half, depth), BF16),
                vmem((2, half, ff), F32),
                vmem((half, ff), BF16),
                vmem((half, depth), BF16),
                vmem((2, half, depth), BF16),
                vmem((tokens, depth), BF16),
                vmem((NBUF, depth // PIECES, ff // 2), BF16),
                vmem((DBUF, ff, depth // PIECES), BF16),
                dma((PIECES,)), dma((NBUF,)), dma((DBUF,)), dma((PIECES,)),
                pltpu.SemaphoreType.REGULAR,
                dma, dma((PIECES,)), dma((3, PIECES)), dma((2, 3, PIECES)),
                dma((4, PIECES)), dma((3, PIECES)), dma((2, PIECES)),
                dma((2,)), dma((2, PIECES)), dma((2, PIECES)), dma((PIECES,)),
                dma((2, PIECES)), dma((2, PIECES)), dma((2, 4, PIECES)), dma((4, PIECES)), dma((PIECES,)),
            ],
            compiler_params=pltpu.CompilerParams(
                collective_id=0, has_side_effects=True, vmem_limit_bytes=67043328),
        )(*(v.reshape(tokens, top).T for v in (expert, slot, gate)),
          x.reshape(tokens, depth), w_gate[0], w_up[0], w_down[0])
        return y.reshape(x.shape)

    tok = P("dp", "ep")
    return jax.shard_map(step, mesh=mesh, in_specs=(tok,) * 4 + (P("ep"),) * 3, out_specs=tok, check_vma=False)
```

time: 155 us -> 119 us (0.77)
  Pallas kernels: 150 us -> 116 us
  other arithmetic: 2.05 us -> 0 us
    pallas_call x1, Pallas kernels: 150 us -> 116 us  [step(): pl.pallas_call(functools.partial(kernel, slots), out_shape=jax.ShapeDtype...]
where the time goes in v2:
time: 119 us; the launch traced here: 118 us
  Pallas kernels  116 us (97%)
  local copies, waits for them, and re-layouts  2.3 us (2%)
    pallas_call x1, Pallas kernels, step(): pl.pallas_call(functools.partial(kernel, slots), out_shape=jax.ShapeDtype...  116 us

profile of v2, /device:TPU:1, one launch (start us, length us, event | category | flops | bytes accessed | tf_op | source)
XLA Modules:
  0.0 118.3 jit_solution(208653076760520685)
XLA Ops:
  0.0 116.0 %shard_map.73 = bf16[256,2048]{1,0:T(8,128)(2,1)} custom-call(s32[2,256]{1,0:T(2,128)} %bitcast.19, s32[2,256]{1,0:T(2,128)} %bitcast.20, f32[2,256]{1,0:T(2,128)} %bitcast.21, bf16[256,2048]{1,0:T(8,128)(2,1)} %bitcast.18, bf16[2048,5632]{1,0:T(8,128)(2,1)} %bitcast.14, bf16[2048,5632]{1,0:T(8,128)(2,1)} %bitcast.15, bf16[5632,2048]{1,0:T(8,128)(2,1)} %bitcast.16), custom_call_target="tpu_custom_call" | custom-call | tf_op jit(solution)/shard_map/pallas_call | solution.py:384
  116.0 2.3 %copy.9 = bf16[1,1,256,2048]{3,2,1,0:T(8,128)(2,1)} copy(bf16[1,1,256,2048]{3,2,1,0:T(8,128)(2,1)} %bitcast.17) | data formatting | bytes 2097152

commit v3 on v2

v3 whole, which is shorter than its diff:
```python
import functools

import jax
import jax.numpy as jnp
from jax import lax
from jax.experimental import pallas as pl
from jax.experimental.pallas import tpu as pltpu
from jax.sharding import PartitionSpec as P

MESH = pl.DeviceIdType.MESH
F32, BF16 = jnp.float32, jnp.bfloat16
PIECES = 4
NBUF = 4
DBUF = 2


def kernel(slots, expert, slot, gate, x_hbm, wg, wu, wd, y_hbm,
           meta, xv, xf, mf, oh, wt, zz, stage, stagef, acc, hbuf, ro, rof,
           part, kbuf, dbuf,
           xsem, ksem, dsem, ysem, go,
           s_meta, s_x, s_own, s_rel, s_far, s_out, s_part,
           r_meta, r_x, r_z, r_zp, r_zn, r_rof, r_ro, r_part):
    S = slots
    T, D = xv.shape
    FF = hbuf.shape[1]
    KT, FT = kbuf.shape[1:]
    NT = dbuf.shape[2]
    C = D // PIECES
    HALF = 4 * S
    NF = FF // FT
    GU = 2 * NF * PIECES

    dp = lax.axis_index("dp")
    me = lax.axis_index("ep")
    z = lax.div(me, 2)
    k = lax.rem(me, 2)
    h = lax.div(me, 4)
    q = lax.rem(me, 4)
    side = lax.rem(z + h + 1, 2)
    mid = side == 0
    end = side == 1
    partner = 2 * z + 1 - k
    qp = partner - 4 * h
    other = 2 + 8 * h - 2 * z
    qo = other - 4 * h
    relay = 4 - 2 * h + k
    far_end = 6 - 6 * h + k
    base = h * HALF
    own = 1 - side

    def rows(i):
        return pl.ds(pl.multiple_of(i * S, 16), S)

    def cols(p):
        return pl.ds(pl.multiple_of(p * C, 128), C)

    def send(src, dst, ssem, rsem, dev):
        return pltpu.make_async_remote_copy(
            src_ref=src, dst_ref=dst, send_sem=ssem, recv_sem=rsem,
            device_id=(dp, dev), device_id_type=MESH)

    def recv(dst, rsem):
        pltpu.make_async_remote_copy(
            src_ref=dst, dst_ref=dst, send_sem=rsem, recv_sem=rsem,
            device_id=(dp, partner), device_id_type=MESH).wait_recv()

    def gu_copy(t, w, m):
        t = lax.rem(t, GU)
        r = pl.ds(pl.multiple_of(lax.div(t, 2 * NF) * KT, 128), KT)
        c = pl.ds(pl.multiple_of(lax.div(lax.rem(t, 2 * NF), 2) * FT, 128), FT)
        return w.at[r, c]

    def gu_start(t):
        s = lax.rem(t, NBUF)

        @pl.when(lax.rem(t, 2) == 0)
        def _():
            pltpu.make_async_copy(gu_copy(t, wg, 0), kbuf.at[s], ksem.at[s]).start()

        @pl.when(lax.rem(t, 2) == 1)
        def _():
            pltpu.make_async_copy(gu_copy(t, wu, 1), kbuf.at[s], ksem.at[s]).start()

    def gu_wait(t):
        s = lax.rem(t, NBUF)
        pltpu.make_async_copy(gu_copy(t, wg, 0), kbuf.at[s], ksem.at[s]).wait()
        return s

    def dn_copy(t):
        s = lax.rem(t, DBUF)
        tile = pl.ds(pl.multiple_of(lax.rem(t, PIECES) * NT, 128), NT)
        return pltpu.make_async_copy(wd.at[:, tile], dbuf.at[s], dsem.at[s])

    xload = [pltpu.make_async_copy(x_hbm.at[:, cols(p)], xv.at[:, cols(p)], xsem.at[p])
             for p in range(PIECES)]
    for c in xload:
        c.start()
    for t in range(NBUF):
        gu_start(jnp.int32(t))
    for t in range(DBUF):
        dn_copy(jnp.int32(t)).start()

    barrier = pltpu.get_barrier_semaphore()

    def greet(d):
        pl.semaphore_signal(barrier, inc=1, device_id=(dp, d), device_id_type=MESH)

    for d in (partner, other, other + 1, relay):
        greet(d)
    pl.when(mid)(lambda: greet(far_end))

    def onehot(m):
        idx = m[...].astype(jnp.int32) - base
        r = lax.broadcasted_iota(jnp.int32, (HALF, T), 0)
        hit = (r == idx[0:1, :]) | (r == idx[1:2, :])
        return jnp.where(hit, 1.0, 0.0).astype(BF16)

    def weights_of(m):
        mt = jnp.transpose(jnp.concatenate([m[...], jnp.zeros((120, T), F32)], axis=0))
        idx = mt.astype(jnp.int32) - base
        r = lax.broadcasted_iota(jnp.int32, (T, HALF), 1)
        w = jnp.where(r == idx[:, 0:1], mt[:, 2:3], 0.0)
        w = jnp.where(r == idx[:, 1:2], mt[:, 3:4], w)
        return w.astype(BF16)

    def dot(a, b):
        return jnp.dot(a, b, preferred_element_type=F32)

    meta[...] = jnp.zeros_like(meta)
    meta[0:2, :] = jnp.where(slot[...] < S, expert[...] * S + slot[...], -100000).astype(F32)
    meta[2:4, :] = gate[...]
    oh[0] = onehot(meta)
    pl.semaphore_wait(barrier, 5 - side)

    send_meta = send(meta, mf.at[side], s_meta, r_meta.at[side], relay)

    def send_x(p):
        return send(xv.at[:, cols(p)], xf.at[side, :, cols(p)], s_x.at[p], r_x.at[side, p], relay)

    def own_copies(p):
        a = send(stage.at[rows(qp), cols(p)], zz.at[own, rows(2 + k), cols(p)], s_own.at[0, p], r_zp.at[p], partner)
        b = [send(stage.at[rows(qo + j), cols(p)], zz.at[own, rows(2 + k), cols(p)], s_own.at[1 + j, p],
                  r_zn.at[k, p], other + j) for j in range(2)]
        return a, b

    send_meta.start()
    for p in range(PIECES):
        xload[p].wait()

        @pl.when(mid)
        def _(p=p):
            send_x(p).start()

    for p in range(PIECES):
        stage[:, cols(p)] = dot(oh[0], xv[:, cols(p)]).astype(BF16)
        a, b = own_copies(p)
        a.start()

        @pl.when(end)
        def _(b=b):
            for c in b:
                c.start()

        zz[own, rows(2 + k), cols(p)] = stage[rows(q), cols(p)]

    def relay_copies(f, p):
        return [send(stagef.at[f, rows(qd), cols(p)], zz.at[f, rows(k), cols(p)], s_rel.at[f, j, p],
                     r_z.at[f, k, p], dev)
                for j, (qd, dev) in enumerate(((qp, partner), (qo, other), (qo + 1, other + 1)))]

    def relay_head(f):
        recv(mf.at[f], r_meta.at[f])
        oh[1 + f] = onehot(mf.at[f])

    def relay_piece(f, p):
        recv(xf.at[f, :, cols(p)], r_x.at[f, p])
        stagef[f, :, cols(p)] = dot(oh[1 + f], xf[f, :, cols(p)]).astype(BF16)
        for c in relay_copies(f, p):
            c.start()
        zz[f, rows(k), cols(p)] = stagef[f, rows(q), cols(p)]

    def await_z(f, p):
        recv(zz.at[f, rows(1 - k), cols(p)], r_z.at[f, 1 - k, p])

        @pl.when(end)
        def _():
            recv(zz.at[f, rows(k), cols(p)], r_z.at[f, k, p])

        @pl.when(own == f)
        def _():
            recv(zz.at[f, rows(3 - k), cols(p)], r_zp.at[p])

        @pl.when(own != f)
        def _():
            for j in range(2):
                recv(zz.at[f, rows(2 + j), cols(p)], r_zn.at[j, p])

    def ft(c):
        return pl.ds(pl.multiple_of(c * FT, 128), FT)

    def gu_next(t):
        @pl.when(t + NBUF < 2 * GU)
        def _():
            gu_start(t + NBUF)

    def gu_piece(f, p):
        t0 = f * GU + p * 2 * NF
        zp = zz.at[f, :, cols(p)]

        @pl.loop(0, NF)
        def _(i):
            if p == 2:
                @pl.when(end & (f == 0) & (i == 1))
                def _():
                    for pp in range(1, PIECES):
                        send_x(pp).start()

            c = ft(i)
            t = t0 + 2 * i
            sg, su = gu_wait(t), gu_wait(t + 1)
            g = dot(zp[...], kbuf[sg])
            if p == 0:
                acc[0, :, c] = g
                acc[1, :, c] = dot(zp[...], kbuf[su])
            elif p < PIECES - 1:
                acc[0, :, c] += g
                acc[1, :, c] += dot(zp[...], kbuf[su])
            else:
                g = acc[0, :, c] + g
                acc[0, :, c] = g * jax.nn.sigmoid(g)
                hbuf[:, c] = (acc[0, :, c] * (acc[1, :, c] + dot(zp[...], kbuf[su]))).astype(BF16)
            gu_next(t)
            gu_next(t + 1)

    def dn_piece(f, p):
        t = f * PIECES + p
        dn_copy(t).wait()
        zz[f, :, cols(p)] = dot(hbuf[...], dbuf[lax.rem(t, DBUF)]).astype(BF16)

        @pl.when(t + DBUF < 2 * PIECES)
        def _():
            dn_copy(t + DBUF).start()

    def out_far(f, p, start):
        def to(kk, dev):
            return send(zz.at[f, rows(kk), cols(p)], rof.at[f, rows(q), cols(p)], s_far.at[f, kk, p],
                        r_rof.at[f, q, p], dev)

        @pl.when(mid)
        def _():
            c = to(1 - k, partner)
            if start:
                c.start()
                rof[f, rows(q), cols(p)] = zz[f, rows(k), cols(p)]
            else:
                c.wait_send()

        @pl.when(end)
        def _():
            for kk in range(2):
                c = to(kk, other + kk)
                c.start() if start else c.wait_send()

    def out_chip(p):
        return send(zz.at[own, rows(3 - k), cols(p)], ro.at[rows(q), cols(p)], s_out.at[0, p], r_ro.at[q, p], partner)

    def out_other(p):
        return [send(zz.at[1 - own, rows(2 + j), cols(p)], ro.at[rows(q), cols(p)], s_out.at[1 + j, p],
                     r_ro.at[q, p], other + j) for j in range(2)]

    def send_part(f, p):
        dev = relay if f == 0 else far_end
        return send(xf.at[f, :, cols(p)], part.at[:, cols(p)], s_part.at[f, p], r_part.at[p], dev)

    def combine_piece(f, p):
        for qq in (qp, qo, qo + 1):
            recv(rof.at[f, rows(qq), cols(p)], r_rof.at[f, qq, p])
        xf[f, :, cols(p)] = dot(wt[1 + f], rof[f, :, cols(p)]).astype(BF16)
        send_part(f, p).start()

    pl.when(mid)(lambda: relay_head(0))

    @pl.loop(0, 2)
    def _(f):
        for p in range(PIECES):
            @pl.when(mid & ((f == 0) | (p < 2)))
            def _(p=p):
                relay_piece(f, p + 2 * f)

            if p == 1:
                @pl.when(mid & (f == 1))
                def _():
                    for pp in range(PIECES):
                        for c in out_other(pp):
                            c.start()

            if p == 2:
                @pl.when(mid & (f == 0))
                def _():
                    pl.semaphore_signal(go, inc=1, device_id=(dp, far_end), device_id_type=MESH)

                @pl.when(end & (f == 0))
                def _():
                    pl.semaphore_wait(go, 1)
                    send_x(0).start()

            if p == 3:
                @pl.when(mid & (f == 0))
                def _():
                    for pp in range(PIECES):
                        for c in own_copies(pp)[1]:
                            c.start()

                @pl.when(mid)
                def _():
                    wt[1 + f] = weights_of(mf.at[f])

            if p > 0:
                @pl.when(mid & (f == 1))
                def _(p=p):
                    combine_piece(0, p - 1)

            await_z(f, p)
            gu_piece(f, p)

        @pl.when(mid & (f == 1))
        def _():
            combine_piece(0, PIECES - 1)

        @pl.loop(0, PIECES)
        def _(p):
            @pl.when(mid & (f == 0) & (p == 0))
            def _():
                relay_head(1)
                relay_piece(1, 0)

            @pl.when(mid & (f == 0) & (p == 2))
            def _():
                relay_piece(1, 1)

            dn_piece(f, p)
            out_far(f, p, True)

            @pl.when(f == own)
            def _():
                out_chip(p).start()
                ro[rows(q), cols(p)] = zz[f, rows(2 + k), cols(p)]

        @pl.when(end & (f == 1))
        def _():
            for p in range(PIECES):
                for c in out_other(p):
                    c.start()

    @pl.when(mid)
    def _():
        for p in range(PIECES):
            combine_piece(1, p)

    wt[0] = weights_of(meta)
    send_meta.wait_send()
    for p in range(PIECES):
        send_x(p).wait_send()
    ycopy = [pltpu.make_async_copy(xv.at[:, cols(p)], y_hbm.at[:, cols(p)], ysem.at[p]) for p in range(PIECES)]
    for p in range(PIECES):
        recv(ro.at[rows(qp), cols(p)], r_ro.at[qp, p])
        for j in range(2):
            recv(ro.at[rows(qo + j), cols(p)], r_ro.at[qo + j, p])
        recv(part.at[:, cols(p)], r_part.at[p])
        xv[:, cols(p)] = (dot(wt[0], ro[:, cols(p)]) + part[:, cols(p)].astype(F32)).astype(BF16)
        ycopy[p].start()

    for p in range(PIECES):
        a, b = own_copies(p)
        for c in (a, *b, out_chip(p), *out_other(p)):
            c.wait_send()
        for f in range(2):
            out_far(f, p, False)

    @pl.when(mid)
    def _():
        for p in range(PIECES):
            for f in range(2):
                for c in relay_copies(f, p):
                    c.wait_send()
                send_part(f, p).wait_send()

    for c in ycopy:
        c.wait()


def solution(mesh):
    def step(x, expert, slot, gate, w_gate, w_up, w_down):
        tokens, depth = x.shape[2:]
        ff = w_gate.shape[2]
        top = expert.shape[3]
        slots = 5 * tokens * top // (4 * 8)
        half = 4 * slots
        dma = pltpu.SemaphoreType.DMA
        vmem = pltpu.VMEM
        hbm = pl.BlockSpec(memory_space=pl.ANY)
        y = pl.pallas_call(
            functools.partial(kernel, slots),
            out_shape=jax.ShapeDtypeStruct((tokens, depth), BF16),
            in_specs=[pl.BlockSpec(memory_space=pltpu.VMEM)] * 3 + [hbm] * 4,
            out_specs=hbm,
            scratch_shapes=[
                vmem((8, tokens), F32),
                vmem((tokens, depth), BF16),
                vmem((2, tokens, depth), BF16),
                vmem((2, 8, tokens), F32),
                vmem((3, half, tokens), BF16),
                vmem((3, tokens, half), BF16),
                vmem((2, half, depth), BF16),
                vmem((half, depth), BF16),
                vmem((2, half, depth), BF16),
                vmem((2, half, ff), F32),
                vmem((half, ff), BF16),
                vmem((half, depth), BF16),
                vmem((2, half, depth), BF16),
                vmem((tokens, depth), BF16),
                vmem((NBUF, depth // PIECES, ff // 2), BF16),
                vmem((DBUF, ff, depth // PIECES), BF16),
                dma((PIECES,)), dma((NBUF,)), dma((DBUF,)), dma((PIECES,)),
                pltpu.SemaphoreType.REGULAR,
                dma, dma((PIECES,)), dma((3, PIECES)), dma((2, 3, PIECES)),
                dma((2, 2, PIECES)), dma((3, PIECES)), dma((2, PIECES)),
                dma((2,)), dma((2, PIECES)), dma((2, 2, PIECES)), dma((PIECES,)), dma((2, PIECES)),
                dma((2, 4, PIECES)), dma((4, PIECES)), dma((PIECES,)),
            ],
            compiler_params=pltpu.CompilerParams(
                collective_id=0, has_side_effects=True, vmem_limit_bytes=67043328),
        )(*(v.reshape(tokens, top).T for v in (expert, slot, gate)),
          x.reshape(tokens, depth), w_gate[0], w_up[0], w_down[0])
        return y.reshape(x.shape)

    tok = P("dp", "ep")
    return jax.shard_map(step, mesh=mesh, in_specs=(tok,) * 4 + (P("ep"),) * 3, out_specs=tok, check_vma=False)
```

time: 119 us -> 110 us (0.924)
  Pallas kernels: 116 us -> 107 us
    pallas_call x1, Pallas kernels: 116 us -> 107 us  [step(): pl.pallas_call(functools.partial(kernel, slots), out_shape=jax.ShapeDtype...]
where the time goes in v3:
time: 110 us
  Pallas kernels  107 us (97%)
  local copies, waits for them, and re-layouts  2.3 us (2%)
    pallas_call x1, Pallas kernels, step(): pl.pallas_call(functools.partial(kernel, slots), out_shape=jax.ShapeDtype...  107 us
    unnamed x1, local copies, waits for them, and re-layouts  2.3 us

profile of v3, /device:TPU:1, one launch (start us, length us, event | category | flops | bytes accessed | tf_op | source)
XLA Modules:
  0.0 109.5 jit_solution(16331862612422804548)
XLA Ops:
  0.0 107.2 %shard_map.73 = bf16[256,2048]{1,0:T(8,128)(2,1)} custom-call(s32[2,256]{1,0:T(2,128)} %bitcast.19, s32[2,256]{1,0:T(2,128)} %bitcast.20, f32[2,256]{1,0:T(2,128)} %bitcast.21, bf16[256,2048]{1,0:T(8,128)(2,1)} %bitcast.18, bf16[2048,5632]{1,0:T(8,128)(2,1)} %bitcast.14, bf16[2048,5632]{1,0:T(8,128)(2,1)} %bitcast.15, bf16[5632,2048]{1,0:T(8,128)(2,1)} %bitcast.16), custom_call_target="tpu_custom_call" | custom-call | tf_op jit(solution)/shard_map/pallas_call | solution.py:402
  107.2 2.3 %copy.9 = bf16[1,1,256,2048]{3,2,1,0:T(8,128)(2,1)} copy(bf16[1,1,256,2048]{3,2,1,0:T(8,128)(2,1)} %bitcast.17) | data formatting | bytes 2097152

commit v4 on v3

--- a/solution.py
+++ b/solution.py
@@ -10,16 +10,17 @@
 MESH = pl.DeviceIdType.MESH
 F32, BF16 = jnp.float32, jnp.bfloat16
 PIECES = 4
+ROWS = 176
 NBUF = 4
 DBUF = 2
 
 
-def kernel(slots, expert, slot, gate, x_hbm, wg, wu, wd, y_hbm,
-           meta, xv, xf, mf, oh, wt, zz, stage, stagef, acc, hbuf, ro, rof,
+def kernel(slots, groups, expert, slot, gate, x_hbm, wg, wu, wd, y_hbm, most,
+           meta, mc, xv, xc, xf, mf, oc, oh, wt, counts, zz, stage, stagef, acc, hbuf, ro, rof,
            part, kbuf, dbuf,
            xsem, ksem, dsem, ysem, go,
            s_meta, s_x, s_own, s_rel, s_far, s_out, s_part,
-           r_meta, r_x, r_z, r_zp, r_zn, r_rof, r_ro, r_part):
+           r_meta, r_x, r_z, r_zp, r_zn, r_rof, r_ro, r_part, s_count, r_count):
     S = slots
     T, D = xv.shape
     FF = hbuf.shape[1]
@@ -46,7 +47,7 @@
     relay = 4 - 2 * h + k
     far_end = 6 - 6 * h + k
     base = h * HALF
-    own = 1 - side
+    block = side * 2 + (1 - side) * (2 + k)
 
     def rows(i):
         return pl.ds(pl.multiple_of(i * S, 16), S)
@@ -103,21 +104,24 @@
     barrier = pltpu.get_barrier_semaphore()
 
     def greet(d):
-        pl.semaphore_signal(barrier, inc=1, device_id=(dp, d), device_id_type=MESH)
-
-    for d in (partner, other, other + 1, relay):
+        pl.semaphore_signal(barrier, inc=1, device_id=d, device_id_type=MESH)
+
+    peers = [(dp, lax.rem(me + d, 8)) for d in range(1, 8)]
+    peers += [(lax.rem(dp + d, groups), me) for d in range(1, groups)]
+    for d in peers:
         greet(d)
-    pl.when(mid)(lambda: greet(far_end))
-
-    def onehot(m):
-        idx = m[...].astype(jnp.int32) - base
+
+    def onehot(m, first):
+        idx = m[...].astype(jnp.int32) - first
         r = lax.broadcasted_iota(jnp.int32, (HALF, T), 0)
         hit = (r == idx[0:1, :]) | (r == idx[1:2, :])
         return jnp.where(hit, 1.0, 0.0).astype(BF16)
 
-    def weights_of(m):
-        mt = jnp.transpose(jnp.concatenate([m[...], jnp.zeros((120, T), F32)], axis=0))
-        idx = mt.astype(jnp.int32) - base
+    def by_token(m):
+        return jnp.transpose(jnp.concatenate([m[...], jnp.zeros((120, T), F32)], axis=0))
+
+    def weights_of(mt, first):
+        idx = mt.astype(jnp.int32) - first
         r = lax.broadcasted_iota(jnp.int32, (T, HALF), 1)
         w = jnp.where(r == idx[:, 0:1], mt[:, 2:3], 0.0)
         w = jnp.where(r == idx[:, 1:2], mt[:, 3:4], w)
@@ -129,23 +133,44 @@
     meta[...] = jnp.zeros_like(meta)
     meta[0:2, :] = jnp.where(slot[...] < S, expert[...] * S + slot[...], -100000).astype(F32)
     meta[2:4, :] = gate[...]
-    oh[0] = onehot(meta)
-    pl.semaphore_wait(barrier, 5 - side)
-
-    send_meta = send(meta, mf.at[side], s_meta, r_meta.at[side], relay)
+    oh[0] = onehot(meta, base)
+
+    far = expert[...] - 4 * (1 - h)
+    there = (far >= 0) & (far < 4) & (slot[...] < S)
+    mc[...] = jnp.zeros_like(mc)
+    mc[0:2, :] = jnp.where(there, far, -4).astype(F32)
+    mc[2:4, :] = jnp.where(there, slot[...], 0).astype(F32)
+    mc[4:6, :] = gate[...]
+    cross = jnp.max(jnp.where(there, 1.0, 0.0), axis=0, keepdims=True)
+    before = lax.broadcasted_iota(jnp.int32, (T, T), 0) < lax.broadcasted_iota(jnp.int32, (T, T), 1)
+    rank = dot(jnp.broadcast_to(cross, (8, T)).astype(BF16), jnp.where(before, 1.0, 0.0).astype(BF16))[0:1, :]
+    rank = jnp.where(cross > 0, rank, -1.0)
+    meta[4:5, :] = rank
+    oc[...] = jnp.where(lax.broadcasted_iota(jnp.int32, (T, T), 0) == rank.astype(jnp.int32), 1.0, 0.0).astype(BF16)
+    m = lax.dot_general(mc[...].astype(BF16), oc[...], (((1,), (1,)), ((), ())), preferred_element_type=F32)
+    mc[0:2, :] = m[0:2, :] * S + m[2:4, :]
+    mc[2:4, :] = m[4:6, :]
+    counts[0] = jnp.broadcast_to(jnp.sum(cross, axis=1, keepdims=True), counts.shape[1:])
+    pl.semaphore_wait(barrier, len(peers))
+
+    send_meta = send(mc, mf.at[side], s_meta, r_meta.at[side], relay)
 
     def send_x(p):
-        return send(xv.at[:, cols(p)], xf.at[side, :, cols(p)], s_x.at[p], r_x.at[side, p], relay)
-
-    def own_copies(p):
-        a = send(stage.at[rows(qp), cols(p)], zz.at[own, rows(2 + k), cols(p)], s_own.at[0, p], r_zp.at[p], partner)
-        b = [send(stage.at[rows(qo + j), cols(p)], zz.at[own, rows(2 + k), cols(p)], s_own.at[1 + j, p],
-                  r_zn.at[k, p], other + j) for j in range(2)]
-        return a, b
+        return send(xc.at[:, cols(p)], xf.at[side, :, cols(p)], s_x.at[p], r_x.at[side, p], relay)
+
+    def own_copy(p):
+        return send(stage.at[rows(qp), cols(p)], zz.at[1, rows(block), cols(p)], s_own.at[0, p], r_zp.at[p], partner)
+
+    def near_copy(j, p):
+        f = (1 - side) * lax.rem(k + j, 2)
+        r = (1 - side) * 3 + side * (2 + k)
+        return send(stage.at[rows(qo + j), cols(p)], zz.at[f, rows(r), cols(p)], s_own.at[1 + j, p],
+                    r_zn.at[k, p], other + j)
 
     send_meta.start()
     for p in range(PIECES):
         xload[p].wait()
+        xc[:, cols(p)] = dot(oc[0:ROWS, :], xv[:, cols(p)]).astype(BF16)
 
         @pl.when(mid)
         def _(p=p):
@@ -153,15 +178,40 @@
 
     for p in range(PIECES):
         stage[:, cols(p)] = dot(oh[0], xv[:, cols(p)]).astype(BF16)
-        a, b = own_copies(p)
-        a.start()
+        own_copy(p).start()
 
         @pl.when(end)
-        def _(b=b):
-            for c in b:
-                c.start()
-
-        zz[own, rows(2 + k), cols(p)] = stage[rows(q), cols(p)]
+        def _(p=p):
+            for j in range(2):
+                near_copy(j, p).start()
+
+        zz[1 - side, rows(block), cols(p)] = stage[rows(q), cols(p)]
+
+    def count_copy(d):
+        if d < 8:
+            return send(counts.at[0], counts.at[d], s_count.at[d], r_count.at[d], lax.rem(me + d, 8))
+        return pltpu.make_async_remote_copy(
+            src_ref=counts.at[11], dst_ref=counts.at[d], send_sem=s_count.at[d], recv_sem=r_count.at[d],
+            device_id=(lax.rem(dp + d - 7, groups), me), device_id_type=MESH)
+
+    for d in range(1, 8):
+        count_copy(d).start()
+
+    def count_group():
+        top = counts[0]
+        for d in range(1, 8):
+            recv(counts.at[d], r_count.at[d])
+            top = jnp.maximum(top, counts[d])
+        counts[11] = top
+        for d in range(8, 7 + groups):
+            count_copy(d).start()
+
+    def count_all():
+        top = counts[11]
+        for d in range(8, 7 + groups):
+            recv(counts.at[d], r_count.at[d])
+            top = jnp.maximum(top, counts[d])
+        most[...] = top
 
     def relay_copies(f, p):
         return [send(stagef.at[f, rows(qd), cols(p)], zz.at[f, rows(k), cols(p)], s_rel.at[f, j, p],
@@ -170,11 +220,11 @@
 
     def relay_head(f):
         recv(mf.at[f], r_meta.at[f])
-        oh[1 + f] = onehot(mf.at[f])
+        oh[1 + f] = onehot(mf.at[f], 0)
 
     def relay_piece(f, p):
         recv(xf.at[f, :, cols(p)], r_x.at[f, p])
-        stagef[f, :, cols(p)] = dot(oh[1 + f], xf[f, :, cols(p)]).astype(BF16)
+        stagef[f, :, cols(p)] = dot(oh[1 + f, :, 0:ROWS], xf[f, :, cols(p)]).astype(BF16)
         for c in relay_copies(f, p):
             c.start()
         zz[f, rows(k), cols(p)] = stagef[f, rows(q), cols(p)]
@@ -186,14 +236,22 @@
         def _():
             recv(zz.at[f, rows(k), cols(p)], r_z.at[f, k, p])
 
-        @pl.when(own == f)
-        def _():
-            recv(zz.at[f, rows(3 - k), cols(p)], r_zp.at[p])
-
-        @pl.when(own != f)
+        @pl.when(mid & (f == 0))
         def _():
             for j in range(2):
                 recv(zz.at[f, rows(2 + j), cols(p)], r_zn.at[j, p])
+
+        @pl.when(mid & (f == 1))
+        def _():
+            recv(zz.at[f, rows(3 - k), cols(p)], r_zp.at[p])
+
+        @pl.when(end & (f == 1))
+        def _():
+            recv(zz.at[f, rows(2), cols(p)], r_zp.at[p])
+
+        @pl.when(end)
+        def _():
+            recv(zz.at[f, rows(3), cols(p)], r_zn.at[lax.rem(k + f, 2), p])
 
     def ft(c):
         return pl.ds(pl.multiple_of(c * FT, 128), FT)
@@ -209,12 +267,6 @@
 
         @pl.loop(0, NF)
         def _(i):
-            if p == 2:
-                @pl.when(end & (f == 0) & (i == 1))
-                def _():
-                    for pp in range(1, PIECES):
-                        send_x(pp).start()
-
             c = ft(i)
             t = t0 + 2 * i
             sg, su = gu_wait(t), gu_wait(t + 1)
@@ -262,11 +314,14 @@
                 c.start() if start else c.wait_send()
 
     def out_chip(p):
-        return send(zz.at[own, rows(3 - k), cols(p)], ro.at[rows(q), cols(p)], s_out.at[0, p], r_ro.at[q, p], partner)
-
-    def out_other(p):
-        return [send(zz.at[1 - own, rows(2 + j), cols(p)], ro.at[rows(q), cols(p)], s_out.at[1 + j, p],
-                     r_ro.at[q, p], other + j) for j in range(2)]
+        r = side * 2 + (1 - side) * (3 - k)
+        return send(zz.at[1, rows(r), cols(p)], ro.at[rows(q), cols(p)], s_out.at[0, p], r_ro.at[q, p], partner)
+
+    def out_other(j, p):
+        f = side * lax.rem(k + j, 2)
+        r = side * 3 + (1 - side) * (2 + j)
+        return send(zz.at[f, rows(r), cols(p)], ro.at[rows(q), cols(p)], s_out.at[1 + j, p],
+                    r_ro.at[q, p], other + j)
 
     def send_part(f, p):
         dev = relay if f == 0 else far_end
@@ -275,7 +330,7 @@
     def combine_piece(f, p):
         for qq in (qp, qo, qo + 1):
             recv(rof.at[f, rows(qq), cols(p)], r_rof.at[f, qq, p])
-        xf[f, :, cols(p)] = dot(wt[1 + f], rof[f, :, cols(p)]).astype(BF16)
+        xf[f, :, cols(p)] = dot(wt[1 + f, 0:ROWS, :], rof[f, :, cols(p)]).astype(BF16)
         send_part(f, p).start()
 
     pl.when(mid)(lambda: relay_head(0))
@@ -283,37 +338,47 @@
     @pl.loop(0, 2)
     def _(f):
         for p in range(PIECES):
-            @pl.when(mid & ((f == 0) | (p < 2)))
-            def _(p=p):
-                relay_piece(f, p + 2 * f)
+            if p < 3:
+                @pl.when(mid & ((f == 0) | (p < 2)))
+                def _(p=p):
+                    early = min(p, 1)
+                    relay_piece(f, (p + early) * (1 - f) + (p + 2) * f)
+                    pl.when(f == 0)(near_copy(k, p + early).start)
+
+            if p < 2:
+                pl.when(mid & (f == 1))(near_copy(1 - k, p + 2).start)
 
             if p == 1:
+                @pl.when(mid & (f == 0))
+                def _():
+                    pl.semaphore_signal(go, inc=1, device_id=(dp, far_end), device_id_type=MESH)
+
+                @pl.when(end & (f == 0))
+                def _():
+                    pl.semaphore_wait(go, 1)
+                    for pp in range(PIECES):
+                        send_x(pp).start()
+
                 @pl.when(mid & (f == 1))
                 def _():
+                    wt[1] = weights_of(by_token(mf.at[0]), 0)
+
+            if p == 2:
+                @pl.when(mid & (f == 1))
+                def _():
                     for pp in range(PIECES):
-                        for c in out_other(pp):
-                            c.start()
-
-            if p == 2:
-                @pl.when(mid & (f == 0))
-                def _():
-                    pl.semaphore_signal(go, inc=1, device_id=(dp, far_end), device_id_type=MESH)
-
-                @pl.when(end & (f == 0))
-                def _():
-                    pl.semaphore_wait(go, 1)
-                    send_x(0).start()
+                        for j in range(2):
+                            out_other(j, pp).start()
 
             if p == 3:
                 @pl.when(mid & (f == 0))
                 def _():
-                    for pp in range(PIECES):
-                        for c in own_copies(pp)[1]:
-                            c.start()
-
-                @pl.when(mid)
-                def _():
-                    wt[1 + f] = weights_of(mf.at[f])
+                    for pp in range(2):
+                        near_copy(1 - k, pp).start()
+
+                @pl.when(mid & (f == 1))
+                def _():
+                    wt[2] = weights_of(by_token(mf.at[1]), 0)
 
             if p > 0:
                 @pl.when(mid & (f == 1))
@@ -321,43 +386,56 @@
                     combine_piece(0, p - 1)
 
             await_z(f, p)
+            if p == 0:
+                @pl.when(mid & (f == 0))
+                def _():
+                    relay_piece(0, 1)
+                    near_copy(k, 1).start()
+
             gu_piece(f, p)
 
         @pl.when(mid & (f == 1))
         def _():
-            combine_piece(0, PIECES - 1)
+            combine_piece(0, 3)
+
+        pl.when(f == 0)(count_group)
 
         @pl.loop(0, PIECES)
         def _(p):
-            @pl.when(mid & (f == 0) & (p == 0))
+            @pl.when(mid & (f == 0) & (p == 1))
             def _():
                 relay_head(1)
                 relay_piece(1, 0)
 
-            @pl.when(mid & (f == 0) & (p == 2))
+            @pl.when(mid & (f == 0) & (p == 3))
             def _():
                 relay_piece(1, 1)
 
             dn_piece(f, p)
             out_far(f, p, True)
 
-            @pl.when(f == own)
+            @pl.when(f == 1)
             def _():
                 out_chip(p).start()
-                ro[rows(q), cols(p)] = zz[f, rows(2 + k), cols(p)]
-
-        @pl.when(end & (f == 1))
+
+            @pl.when(f == 1 - side)
+            def _():
+                ro[rows(q), cols(p)] = zz[f, rows(block), cols(p)]
+
+        @pl.when(end)
         def _():
             for p in range(PIECES):
-                for c in out_other(p):
-                    c.start()
+                out_other(lax.rem(k + f, 2), p).start()
 
     @pl.when(mid)
     def _():
         for p in range(PIECES):
             combine_piece(1, p)
 
-    wt[0] = weights_of(meta)
+    count_all()
+    mt = by_token(meta)
+    wt[0] = weights_of(mt, base)
+    oc[...] = jnp.where(lax.broadcasted_iota(jnp.int32, (T, T), 1) == mt[:, 4:5].astype(jnp.int32), 1.0, 0.0).astype(BF16)
     send_meta.wait_send()
     for p in range(PIECES):
         send_x(p).wait_send()
@@ -367,12 +445,11 @@
         for j in range(2):
             recv(ro.at[rows(qo + j), cols(p)], r_ro.at[qo + j, p])
         recv(part.at[:, cols(p)], r_part.at[p])
-        xv[:, cols(p)] = (dot(wt[0], ro[:, cols(p)]) + part[:, cols(p)].astype(F32)).astype(BF16)
+        xv[:, cols(p)] = (dot(wt[0], ro[:, cols(p)]) + dot(oc[:, 0:ROWS], part[:, cols(p)])).astype(BF16)
         ycopy[p].start()
 
     for p in range(PIECES):
-        a, b = own_copies(p)
-        for c in (a, *b, out_chip(p), *out_other(p)):
+        for c in (own_copy(p), near_copy(0, p), near_copy(1, p), out_chip(p), out_other(0, p), out_other(1, p)):
             c.wait_send()
         for f in range(2):
             out_far(f, p, False)
@@ -385,6 +462,8 @@
                     c.wait_send()
                 send_part(f, p).wait_send()
 
+    for d in range(1, 7 + groups):
+        count_copy(d).wait_send()
     for c in ycopy:
         c.wait()
 
@@ -399,18 +478,25 @@
         dma = pltpu.SemaphoreType.DMA
         vmem = pltpu.VMEM
         hbm = pl.BlockSpec(memory_space=pl.ANY)
-        y = pl.pallas_call(
-            functools.partial(kernel, slots),
-            out_shape=jax.ShapeDtypeStruct((tokens, depth), BF16),
+        routing = [v.reshape(tokens, top) for v in (expert, slot, gate)]
+        x2, wg, wu, wd = x.reshape(tokens, depth), w_gate[0], w_up[0], w_down[0]
+        groups = mesh.shape["dp"]
+        y, most = pl.pallas_call(
+            functools.partial(kernel, slots, groups),
+            out_shape=(jax.ShapeDtypeStruct((tokens, depth), BF16), jax.ShapeDtypeStruct((8, 128), F32)),
             in_specs=[pl.BlockSpec(memory_space=pltpu.VMEM)] * 3 + [hbm] * 4,
-            out_specs=hbm,
+            out_specs=(hbm, pl.BlockSpec(memory_space=pltpu.VMEM)),
             scratch_shapes=[
                 vmem((8, tokens), F32),
+                vmem((8, tokens), F32),
                 vmem((tokens, depth), BF16),
-                vmem((2, tokens, depth), BF16),
+                vmem((ROWS, depth), BF16),
+                vmem((2, ROWS, depth), BF16),
                 vmem((2, 8, tokens), F32),
+                vmem((tokens, tokens), BF16),
                 vmem((3, half, tokens), BF16),
                 vmem((3, tokens, half), BF16),
+                vmem((12, 8, 128), F32),
                 vmem((2, half, depth), BF16),
                 vmem((half, depth), BF16),
                 vmem((2, half, depth), BF16),
@@ -418,7 +504,7 @@
                 vmem((half, ff), BF16),
                 vmem((half, depth), BF16),
                 vmem((2, half, depth), BF16),
-                vmem((tokens, depth), BF16),
+                vmem((ROWS, depth), BF16),
                 vmem((NBUF, depth // PIECES, ff // 2), BF16),
                 vmem((DBUF, ff, depth // PIECES), BF16),
                 dma((PIECES,)), dma((NBUF,)), dma((DBUF,)), dma((PIECES,)),
@@ -426,12 +512,28 @@
                 dma, dma((PIECES,)), dma((3, PIECES)), dma((2, 3, PIECES)),
                 dma((2, 2, PIECES)), dma((3, PIECES)), dma((2, PIECES)),
                 dma((2,)), dma((2, PIECES)), dma((2, 2, PIECES)), dma((PIECES,)), dma((2, PIECES)),
-                dma((2, 4, PIECES)), dma((4, PIECES)), dma((PIECES,)),
+                dma((2, 4, PIECES)), dma((4, PIECES)), dma((PIECES,)), dma((11,)), dma((11,)),
             ],
             compiler_params=pltpu.CompilerParams(
                 collective_id=0, has_side_effects=True, vmem_limit_bytes=67043328),
-        )(*(v.reshape(tokens, top).T for v in (expert, slot, gate)),
-          x.reshape(tokens, depth), w_gate[0], w_up[0], w_down[0])
+        )(*(v.T for v in routing), x2, wg, wu, wd)
+
+        def dot(a, b):
+            return jnp.dot(a, b, preferred_element_type=F32)
+
+        def every_slot():
+            e, c, g = routing
+            place = jnp.where(c < slots, e * slots + c, -1)
+            hit = place[:, :, None] == jnp.arange(8 * slots)
+            gates = jnp.where(hit, g.astype(BF16)[:, :, None], jnp.zeros((), BF16))
+            z = dot(jnp.any(hit, axis=1).astype(BF16).T, x2).astype(BF16)
+            z = lax.all_to_all(z.reshape(8, slots, depth), "ep", 0, 0).reshape(8 * slots, depth)
+            u = (jax.nn.silu(dot(z, wg)) * dot(z, wu)).astype(BF16)
+            out = dot(u, wd).astype(BF16).reshape(8, slots, depth)
+            out = lax.all_to_all(out, "ep", 0, 0).reshape(8 * slots, depth)
+            return dot(jnp.sum(gates, axis=1), out).astype(BF16)
+
+        y = lax.cond(most[0, 0] > ROWS, every_slot, lambda: y)
         return y.reshape(x.shape)
 
     tok = P("dp", "ep")

time: 110 us -> 99.6 us (0.905)
  Pallas kernels: 107 us -> 95.1 us
  local copies, waits for them, and re-layouts: 2.3 us -> 3.49 us
    pallas_call x1, Pallas kernels: 107 us -> 95.1 us  [step(): pl.pallas_call(functools.partial(kernel, slots, groups), out_shape=(jax.S...]
    slice x0 -> x1, local copies, waits for them, and re-layouts: none -> 1.18 us  [step(): y = lax.cond(most[0, 0] > ROWS, every_slot, lambda: y)]
where the time goes in v4:
time: 99.6 us; the launch traced here: 99.3 us
  Pallas kernels  95.1 us (95%)
  local copies, waits for them, and re-layouts  3.49 us (4%)
    pallas_call x1, Pallas kernels, step(): pl.pallas_call(functools.partial(kernel, slots, groups), out_shape=(jax.S...  95.1 us
    unnamed x1, local copies, waits for them, and re-layouts  2.3 us

profile of v4, /device:TPU:1, one launch (start us, length us, event | category | flops | bytes accessed | tf_op | source)
XLA Modules:
  0.0 99.3 jit_solution(7026785912281619450)
XLA Ops:
  0.0 95.1 %shard_map.75 = (bf16[256,2048]{1,0:T(8,128)(2,1)}, f32[8,128]{1,0:T(8,128)}) custom-call(s32[2,256]{1,0:T(2,128)} %bitcast.52, s32[2,256]{1,0:T(2,128)} %bitcast.54, f32[2,256]{1,0:T(2,128)} %bitcast.56, bf16[256,2048]{1,0:T(8,128)(2,1)} %bitcast.46, bf16[2048,5632]{1,0:T(8,128)(2,1)} %bitcast.38, bf16[2048,5632]{1,0:T(8,128)(2,1)} %bitcast.40, ...), custom_call_target="tpu_custom_call" | custom-call | tf_op jit(solution)/shard_map/pallas_call | solution.py:484
  95.2 1.2 %slice.3 = f32[1,1]{1,0:T(1,128)} slice(f32[8,128]{1,0:T(8,128)} %get-tuple-element.34), slice={[0:1], [0:1]} | slice | bytes 8 | tf_op jit(solution)/shard_map/slice | solution.py:536
  97.0 2.3 %copy.15 = bf16[1,1,256,2048]{3,2,1,0:T(8,128)(2,1)} copy(bf16[1,1,256,2048]{3,2,1,0:T(8,128)(2,1)} %get-tuple-element.36) | data formatting | bytes 2097152
  (1 shorter events, 0.0 us)

commit v5 on v4

--- a/solution.py
+++ b/solution.py
@@ -15,7 +15,7 @@
 DBUF = 2
 
 
-def kernel(slots, groups, expert, slot, gate, x_hbm, wg, wu, wd, y_hbm, most,
+def kernel(slots, groups, expert, slot, gate, x_hbm, wg, wu, wd, y_hbm, over,
            meta, mc, xv, xc, xf, mf, oc, oh, wt, counts, zz, stage, stagef, acc, hbuf, ro, rof,
            part, kbuf, dbuf,
            xsem, ksem, dsem, ysem, go,
@@ -106,10 +106,11 @@
     def greet(d):
         pl.semaphore_signal(barrier, inc=1, device_id=d, device_id_type=MESH)
 
-    peers = [(dp, lax.rem(me + d, 8)) for d in range(1, 8)]
+    peers = [(dp, d) for d in (partner, other, other + 1, relay)]
     peers += [(lax.rem(dp + d, groups), me) for d in range(1, groups)]
     for d in peers:
         greet(d)
+    pl.when(mid)(lambda: greet((dp, far_end)))
 
     def onehot(m, first):
         idx = m[...].astype(jnp.int32) - first
@@ -151,7 +152,7 @@
     mc[0:2, :] = m[0:2, :] * S + m[2:4, :]
     mc[2:4, :] = m[4:6, :]
     counts[0] = jnp.broadcast_to(jnp.sum(cross, axis=1, keepdims=True), counts.shape[1:])
-    pl.semaphore_wait(barrier, len(peers))
+    pl.semaphore_wait(barrier, len(peers) + 1 - side)
 
     send_meta = send(mc, mf.at[side], s_meta, r_meta.at[side], relay)
 
@@ -168,16 +169,21 @@
                     r_zn.at[k, p], other + j)
 
     send_meta.start()
+    def pack_x(p):
+        xc[:, cols(p)] = dot(oc[0:ROWS, :], xv[:, cols(p)]).astype(BF16)
+
     for p in range(PIECES):
         xload[p].wait()
-        xc[:, cols(p)] = dot(oc[0:ROWS, :], xv[:, cols(p)]).astype(BF16)
 
         @pl.when(mid)
         def _(p=p):
+            pack_x(p)
             send_x(p).start()
 
     for p in range(PIECES):
         stage[:, cols(p)] = dot(oh[0], xv[:, cols(p)]).astype(BF16)
+        if p < 2:
+            pl.when(mid)(near_copy(k, p).start)
         own_copy(p).start()
 
         @pl.when(end)
@@ -187,31 +193,46 @@
 
         zz[1 - side, rows(block), cols(p)] = stage[rows(q), cols(p)]
 
-    def count_copy(d):
-        if d < 8:
-            return send(counts.at[0], counts.at[d], s_count.at[d], r_count.at[d], lax.rem(me + d, 8))
+    @pl.when(end)
+    def _():
+        for p in range(PIECES):
+            pack_x(p)
+
+    def count_copy(src, dst, i, dev):
         return pltpu.make_async_remote_copy(
-            src_ref=counts.at[11], dst_ref=counts.at[d], send_sem=s_count.at[d], recv_sem=r_count.at[d],
-            device_id=(lax.rem(dp + d - 7, groups), me), device_id_type=MESH)
-
-    for d in range(1, 8):
-        count_copy(d).start()
-
-    def count_group():
-        top = counts[0]
-        for d in range(1, 8):
+            src_ref=counts.at[src], dst_ref=counts.at[dst], send_sem=s_count.at[i], recv_sem=r_count.at[dst],
+            device_id=dev, device_id_type=MESH)
+
+    count_half = [count_copy(0, 1, 1, (dp, partner)), count_copy(0, 2 + k, 2, (dp, other)),
+                  count_copy(0, 2 + k, 3, (dp, other + 1))]
+    count_over = [count_copy(4, 5, 4, (dp, relay)), count_copy(4, 5, 5, (dp, far_end))]
+    count_dp = [count_copy(6, 6 + d, 5 + d, (lax.rem(dp + d, groups), me)) for d in range(1, groups)]
+    for c in count_half:
+        c.start()
+
+    def largest(i, slots):
+        top = counts[i]
+        for d in slots:
             recv(counts.at[d], r_count.at[d])
             top = jnp.maximum(top, counts[d])
-        counts[11] = top
-        for d in range(8, 7 + groups):
-            count_copy(d).start()
+        return top
+
+    def count_far():
+        counts[4] = largest(0, (1, 2, 3))
+
+        @pl.when(mid)
+        def _():
+            for c in count_over:
+                c.start()
+
+    def count_group():
+        counts[6] = largest(4, (5,))
+        for c in count_dp:
+            c.start()
 
     def count_all():
-        top = counts[11]
-        for d in range(8, 7 + groups):
-            recv(counts.at[d], r_count.at[d])
-            top = jnp.maximum(top, counts[d])
-        most[...] = top
+        top = largest(6, range(7, 6 + groups))
+        over[0, 0] = (jnp.max(top) > ROWS).astype(jnp.int32)
 
     def relay_copies(f, p):
         return [send(stagef.at[f, rows(qd), cols(p)], zz.at[f, rows(k), cols(p)], s_rel.at[f, j, p],
@@ -343,7 +364,8 @@
                 def _(p=p):
                     early = min(p, 1)
                     relay_piece(f, (p + early) * (1 - f) + (p + 2) * f)
-                    pl.when(f == 0)(near_copy(k, p + early).start)
+                    if p == 1:
+                        pl.when(f == 0)(near_copy(k, 3).start)
 
             if p < 2:
                 pl.when(mid & (f == 1))(near_copy(1 - k, p + 2).start)
@@ -390,7 +412,7 @@
                 @pl.when(mid & (f == 0))
                 def _():
                     relay_piece(0, 1)
-                    near_copy(k, 1).start()
+                    near_copy(k, 2).start()
 
             gu_piece(f, p)
 
@@ -398,7 +420,8 @@
         def _():
             combine_piece(0, 3)
 
-        pl.when(f == 0)(count_group)
+        pl.when(f == 0)(count_far)
+        pl.when(f == 1)(count_group)
 
         @pl.loop(0, PIECES)
         def _(p):
@@ -411,6 +434,10 @@
             def _():
                 relay_piece(1, 1)
 
+            @pl.when(mid & (f == 1) & (p == 3))
+            def _():
+                combine_piece(1, 0)
+
             dn_piece(f, p)
             out_far(f, p, True)
 
@@ -429,7 +456,7 @@
 
     @pl.when(mid)
     def _():
-        for p in range(PIECES):
+        for p in range(1, PIECES):
             combine_piece(1, p)
 
     count_all()
@@ -462,9 +489,29 @@
                     c.wait_send()
                 send_part(f, p).wait_send()
 
-    for d in range(1, 7 + groups):
-        count_copy(d).wait_send()
+    for c in (*count_half, *count_dp):
+        c.wait_send()
+
+    @pl.when(mid)
+    def _():
+        for c in count_over:
+            c.wait_send()
+
     for c in ycopy:
+        c.wait()
+
+
+def copy_kernel(src, dst, buf, isem, osem):
+    n = buf.shape[0] // PIECES
+    parts = [pl.ds(i * n, n) for i in range(PIECES)]
+    load = [pltpu.make_async_copy(src.at[r], buf.at[r], isem.at[i]) for i, r in enumerate(parts)]
+    save = [pltpu.make_async_copy(buf.at[r], dst.at[r], osem.at[i]) for i, r in enumerate(parts)]
+    for c in load:
+        c.start()
+    for a, b in zip(load, save):
+        a.wait()
+        b.start()
+    for c in save:
         c.wait()
 
 
@@ -481,11 +528,11 @@
         routing = [v.reshape(tokens, top) for v in (expert, slot, gate)]
         x2, wg, wu, wd = x.reshape(tokens, depth), w_gate[0], w_up[0], w_down[0]
         groups = mesh.shape["dp"]
-        y, most = pl.pallas_call(
+        y, over = pl.pallas_call(
             functools.partial(kernel, slots, groups),
-            out_shape=(jax.ShapeDtypeStruct((tokens, depth), BF16), jax.ShapeDtypeStruct((8, 128), F32)),
+            out_shape=(jax.ShapeDtypeStruct((tokens, depth), BF16), jax.ShapeDtypeStruct((1, 1), jnp.int32)),
             in_specs=[pl.BlockSpec(memory_space=pltpu.VMEM)] * 3 + [hbm] * 4,
-            out_specs=(hbm, pl.BlockSpec(memory_space=pltpu.VMEM)),
+            out_specs=(hbm, pl.BlockSpec(memory_space=pltpu.SMEM)),
             scratch_shapes=[
                 vmem((8, tokens), F32),
                 vmem((8, tokens), F32),
@@ -533,7 +580,13 @@
             out = lax.all_to_all(out, "ep", 0, 0).reshape(8 * slots, depth)
             return dot(jnp.sum(gates, axis=1), out).astype(BF16)
 
-        y = lax.cond(most[0, 0] > ROWS, every_slot, lambda: y)
+        def pass_on():
+            return pl.pallas_call(
+                copy_kernel, out_shape=jax.ShapeDtypeStruct(y.shape, BF16), in_specs=[hbm], out_specs=hbm,
+                scratch_shapes=[vmem(y.shape, BF16), dma((PIECES,)), dma((PIECES,))],
+            )(y)
+
+        y = lax.switch(over[0, 0], (pass_on, every_slot))
         return y.reshape(x.shape)
 
     tok = P("dp", "ep")

time: 99.6 us -> 95 us (0.954)
  local copies, waits for them, and re-layouts: 3.49 us -> 0 us
  Pallas kernels: 95.1 us -> 93.9 us
    pallas_call x1, Pallas kernels: 95.1 us -> 92 us  [step(): pl.pallas_call(functools.partial(kernel, slots, groups), out_shape=(jax.S...]
    unnamed x1 -> x0, local copies, waits for them, and re-layouts: 2.3 us -> none
    pallas_call x0 -> x1, Pallas kernels: none -> 1.98 us  [pass_on(): pl.pallas_call(copy_kernel, out_shape=jax.ShapeDtypeStruct(y.shape, BF16)...]
    slice x1 -> x0, local copies, waits for them, and re-layouts: 1.18 us -> none  [step(): y = lax.cond(most[0, 0] > ROWS, every_slot, lambda: y)]
where the time goes in v5:
time: 95 us; the launch traced here: 94.7 us
  Pallas kernels  93.9 us (99%)
    pallas_call x1, Pallas kernels, step(): pl.pallas_call(functools.partial(kernel, slots, groups), out_shape=(jax.S...  92 us
    pallas_call x1, Pallas kernels, pass_on(): pl.pallas_call(copy_kernel, out_shape=jax.ShapeDtypeStruct(y.shape, BF16)...  1.98 us

profile of v5, /device:TPU:1, one launch (start us, length us, event | category | flops | bytes accessed | tf_op | source)
XLA Modules:
  0.0 94.7 jit_solution(3207641012150443119)
XLA Ops:
  0.0 92.0 %shard_map.75 = (bf16[256,2048]{1,0:T(8,128)(2,1)}, s32[1,1]{1,0:T(1,128)}) custom-call(s32[2,256]{1,0:T(2,128)} %bitcast.51, s32[2,256]{1,0:T(2,128)} %bitcast.53, f32[2,256]{1,0:T(2,128)} %bitcast.55, bf16[256,2048]{1,0:T(8,128)(2,1)} %bitcast.46, bf16[2048,5632]{1,0:T(8,128)(2,1)} %bitcast.38, bf16[2048,5632]{1,0:T(8,128)(2,1)} %bitcast.40, ...), custom_call_target="tpu_custom_call" | custom-call | tf_op jit(solution)/shard_map/pallas_call | solution.py:531
  92.5 2.0 %conditional.1 = (bf16[1,1,256,2048]{3,2,1,0:T(8,128)(2,1)}) conditional(s32[]{:T(128)} %bitcast.16, bf16[256,2048]{1,0:T(8,128)(2,1)} %get-tuple-element.34, (s32[256,2]{0,1:T(2,128)}, s32[256,2]{0,1:T(2,128)}, f32[256,2]{0,1:T(2,128)}, bf16[256,2048]{1,0:T(8,128)(2,1)}, bf16[2048,5632]{1,0:T(8,128)(2,1)}, /*index=5*/bf16[2048,5632]{1,0:T(8,128)(2,1)}, ...), branch_computations={%region_0.0_spmd, %region_1.4_spmd} | conditional | flops 45660110848 | bytes 141776960 | solution.py:589
  92.5 2.0 %branch_0_fun.1 = bf16[256,2048]{1,0:T(8,128)(2,1)} custom-call(bf16[256,2048]{1,0:T(8,128)(2,1)} %src), custom_call_target="tpu_custom_call" | custom-call | tf_op jit(solution)/shard_map/cond/branch_0_fun/pallas_call | solution.py:584

commit v6 on v5

--- a/solution.py
+++ b/solution.py
@@ -10,6 +10,7 @@
 MESH = pl.DeviceIdType.MESH
 F32, BF16 = jnp.float32, jnp.bfloat16
 PIECES = 4
+COPIES = 2
 ROWS = 176
 NBUF = 4
 DBUF = 2
@@ -182,7 +183,7 @@
 
     for p in range(PIECES):
         stage[:, cols(p)] = dot(oh[0], xv[:, cols(p)]).astype(BF16)
-        if p < 2:
+        if p < 1:
             pl.when(mid)(near_copy(k, p).start)
         own_copy(p).start()
 
@@ -364,17 +365,13 @@
                 def _(p=p):
                     early = min(p, 1)
                     relay_piece(f, (p + early) * (1 - f) + (p + 2) * f)
-                    if p == 1:
-                        pl.when(f == 0)(near_copy(k, 3).start)
+                    if p != 2:
+                        pl.when(f == 0)(near_copy(k, 2 * p + 1).start)
 
             if p < 2:
                 pl.when(mid & (f == 1))(near_copy(1 - k, p + 2).start)
 
             if p == 1:
-                @pl.when(mid & (f == 0))
-                def _():
-                    pl.semaphore_signal(go, inc=1, device_id=(dp, far_end), device_id_type=MESH)
-
                 @pl.when(end & (f == 0))
                 def _():
                     pl.semaphore_wait(go, 1)
@@ -412,6 +409,7 @@
                 @pl.when(mid & (f == 0))
                 def _():
                     relay_piece(0, 1)
+                    pl.semaphore_signal(go, inc=1, device_id=(dp, far_end), device_id_type=MESH)
                     near_copy(k, 2).start()
 
             gu_piece(f, p)
@@ -471,8 +469,11 @@
         recv(ro.at[rows(qp), cols(p)], r_ro.at[qp, p])
         for j in range(2):
             recv(ro.at[rows(qo + j), cols(p)], r_ro.at[qo + j, p])
+        acc[0, 0:T, cols(p)] = dot(wt[0], ro[:, cols(p)])
+
+    for p in range(PIECES):
         recv(part.at[:, cols(p)], r_part.at[p])
-        xv[:, cols(p)] = (dot(wt[0], ro[:, cols(p)]) + dot(oc[:, 0:ROWS], part[:, cols(p)])).astype(BF16)
+        xv[:, cols(p)] = (acc[0, 0:T, cols(p)] + dot(oc[:, 0:ROWS], part[:, cols(p)])).astype(BF16)
         ycopy[p].start()
 
     for p in range(PIECES):
@@ -502,8 +503,8 @@
 
 
 def copy_kernel(src, dst, buf, isem, osem):
-    n = buf.shape[0] // PIECES
-    parts = [pl.ds(i * n, n) for i in range(PIECES)]
+    n = buf.shape[0] // COPIES
+    parts = [pl.ds(i * n, n) for i in range(COPIES)]
     load = [pltpu.make_async_copy(src.at[r], buf.at[r], isem.at[i]) for i, r in enumerate(parts)]
     save = [pltpu.make_async_copy(buf.at[r], dst.at[r], osem.at[i]) for i, r in enumerate(parts)]
     for c in load:
@@ -583,7 +584,7 @@
         def pass_on():
             return pl.pallas_call(
                 copy_kernel, out_shape=jax.ShapeDtypeStruct(y.shape, BF16), in_specs=[hbm], out_specs=hbm,
-                scratch_shapes=[vmem(y.shape, BF16), dma((PIECES,)), dma((PIECES,))],
+                scratch_shapes=[vmem(y.shape, BF16), dma((COPIES,)), dma((COPIES,))],
             )(y)
 
         y = lax.switch(over[0, 0], (pass_on, every_slot))

time: 95 us -> 94.8 us (level)
  no operation moved by 1% of the time
where the time goes in v6:
time: 94.8 us; the launch traced here: 94.6 us
  Pallas kernels  93.8 us (99%)
    pallas_call x1, Pallas kernels, step(): pl.pallas_call(functools.partial(kernel, slots, groups), out_shape=(jax.S...  91.8 us
    pallas_call x1, Pallas kernels, pass_on(): pl.pallas_call(copy_kernel, out_shape=jax.ShapeDtypeStruct(y.shape, BF16)...  2.04 us

profile of v6, /device:TPU:1, one launch (start us, length us, event | category | flops | bytes accessed | tf_op | source)
XLA Modules:
  0.0 94.6 jit_solution(15996372815717981798)
XLA Ops:
  0.0 91.8 %shard_map.75 = (bf16[256,2048]{1,0:T(8,128)(2,1)}, s32[1,1]{1,0:T(1,128)}) custom-call(s32[2,256]{1,0:T(2,128)} %bitcast.51, s32[2,256]{1,0:T(2,128)} %bitcast.53, f32[2,256]{1,0:T(2,128)} %bitcast.55, bf16[256,2048]{1,0:T(8,128)(2,1)} %bitcast.46, bf16[2048,5632]{1,0:T(8,128)(2,1)} %bitcast.38, bf16[2048,5632]{1,0:T(8,128)(2,1)} %bitcast.40, ...), custom_call_target="tpu_custom_call" | custom-call | tf_op jit(solution)/shard_map/pallas_call | solution.py:532
  92.3 2.1 %conditional.1 = (bf16[1,1,256,2048]{3,2,1,0:T(8,128)(2,1)}) conditional(s32[]{:T(128)} %bitcast.16, bf16[256,2048]{1,0:T(8,128)(2,1)} %get-tuple-element.34, (s32[256,2]{0,1:T(2,128)}, s32[256,2]{0,1:T(2,128)}, f32[256,2]{0,1:T(2,128)}, bf16[256,2048]{1,0:T(8,128)(2,1)}, bf16[2048,5632]{1,0:T(8,128)(2,1)}, /*index=5*/bf16[2048,5632]{1,0:T(8,128)(2,1)}, ...), branch_computations={%region_0.0_spmd, %region_1.4_spmd} | conditional | flops 45660110848 | bytes 141776960 | solution.py:590
  92.3 2.0 %branch_0_fun.1 = bf16[256,2048]{1,0:T(8,128)(2,1)} custom-call(bf16[256,2048]{1,0:T(8,128)(2,1)} %src), custom_call_target="tpu_custom_call" | custom-call | tf_op jit(solution)/shard_map/cond/branch_0_fun/pallas_call | solution.py:585
